TPU v7x, 8 devices: a whole 2x2x1 slice. The times are simulated.
8 devices in a mesh: dp: 4 (over z, y, x), ep: 2 (over core).
Axes of the slice: x: 2, y: 2, z: 1, core: 2. Of those that a mesh axis runs over, the one named last changes fastest.
Arguments:
- x_norm: bfloat16 [2048, 1024], P(('dp', 'ep'))
- route_idx: int32 [2048, 8], P(('dp', 'ep'))
- w_router: bfloat16 [1024, 32], replicated
- w_gate: bfloat16 [32, 1024, 512], P('ep')
- w_up: bfloat16 [32, 1024, 512], P('ep')
- w_down: bfloat16 [32, 512, 1024], P('ep')
- grad_out: bfloat16 [2048, 1024], P(('dp', 'ep'))
Outputs:
- output 1: bfloat16 [2048, 1024], P(('dp', 'ep'))
- output 2: float32 [32, 1024, 512], P('ep')
- output 3: float32 [32, 1024, 512], P('ep')
- output 4: float32 [32, 512, 1024], P('ep')
- output 5: float32 [1024, 32], replicated
All inputs are finite; a program needn't handle non-finite values.
Results may differ from a plain program's by a relative error of at most 0.00616128.
Values are sent between devices in bfloat16 or wider.
A program may use at most 1 GiB of HBM per device.

v0:
```python
import functools

import jax
import jax.numpy as jnp
from jax import lax
from jax.experimental import pallas as pl
from jax.experimental.pallas import tpu as pltpu
from jax.sharding import PartitionSpec as P

D = 1024
FF = 512
EXPERTS = 32
TOP = 8
TOK = 256
SHARDS = 8
E_LOC = 16
SLOT = 64
GROUP = 4
ROWS = SHARDS * SLOT
HOT = 128
CAP = 192
F32 = jnp.float32
BF16 = jnp.bfloat16


def dot_nn(a, b):
    return lax.dot_general(a, b, (((1,), (0,)), ((), ())), preferred_element_type=F32)


def dot_nt(a, b):
    return lax.dot_general(a, b, (((1,), (1,)), ((), ())), preferred_element_type=F32)


def dot_tn(a, b):
    return lax.dot_general(a, b, (((0,), (0,)), ((), ())), preferred_element_type=F32)


def route_tables(x_s, idx_t, w_router):
    logits = lax.dot_general(w_router, x_s, (((0,), (1,)), ((), ())), preferred_element_type=F32)
    e_iota = lax.broadcasted_iota(jnp.int32, (EXPERTS, TOK), 0)
    mask = e_iota == idx_t[0:1, :]
    for k in range(1, TOP):
        mask = mask | (e_iota == idx_t[k:k + 1, :])
    top = jnp.max(jnp.where(mask, logits, -jnp.inf), axis=0, keepdims=True)
    ex = jnp.where(mask, jnp.exp(jnp.where(mask, logits - top, 0.0)), 0.0)
    gates = ex / jnp.sum(ex, axis=0, keepdims=True)
    mask_f = jnp.where(mask, 1.0, 0.0)
    before = lax.broadcasted_iota(jnp.int32, (TOK, TOK), 0) < lax.broadcasted_iota(jnp.int32, (TOK, TOK), 1)
    rank = dot_nn(mask_f.astype(BF16), jnp.where(before, 1.0, 0.0).astype(BF16))
    code = jnp.where(mask, rank, -1.0)
    count = jnp.sum(mask_f, axis=1, keepdims=True)
    return code, gates, count


def main_kernel(info, x_ref, g_ref, idx_ref, wr_ref, w1_ref, w3_ref, w2_ref,
                o1_ref, o3_ref, o2_ref, s_ref, q_ref, gate_ref,
                code_s, gate_s, hot_s, list_s, xg_s, do_s, gg_s, r_s, a_s, dz1_s, dz3_s):
    i = pl.program_id(0)
    core = info[0]
    dp = info[1]
    e = core * E_LOC + i
    j = lax.rem(i, GROUP)

    def shard_of(b):
        return lax.rem(2 * dp + b, SHARDS)

    def slot_mask(b, ex, rows, base):
        row = code_s[b, pl.ds(ex, 1), :] - base
        r_iota = lax.broadcasted_iota(jnp.int32, (rows, TOK), 0).astype(F32)
        return row == r_iota

    def as_bf16(mask):
        return jnp.where(mask, 1.0, 0.0).astype(BF16)

    @pl.when(i == 0)
    def _():
        def prep(b, _):
            s = shard_of(b)
            code, gates, count = route_tables(x_ref[s], idx_ref[s], wr_ref[...])
            code_s[b] = code
            gate_s[b] = gates
            e_col = lax.broadcasted_iota(jnp.int32, (EXPERTS, 1), 0).astype(F32)
            hot_s[b] = jnp.max(jnp.where(count > SLOT, e_col, -1.0)).astype(jnp.int32)
            return 0
        lax.fori_loop(0, SHARDS, prep, 0)
        for b in range(2):
            gate_ref[b] = gate_s[b]
        s_ref[...] = jnp.zeros_like(s_ref)

    @pl.when(j == 0)
    def _():
        def gather(b, _):
            s = shard_of(b)
            masks = [slot_mask(b, e + jj, SLOT, 0.0) for jj in range(GROUP)]
            sel = jnp.concatenate([as_bf16(m) for m in masks], axis=0)
            xg = dot_nn(sel, x_ref[s]).astype(BF16)
            gg = dot_nn(sel, g_ref[s])
            row0 = pl.multiple_of(b * SLOT, SLOT)
            for jj in range(GROUP):
                part = slice(jj * SLOT, (jj + 1) * SLOT)
                xg_s[jj, pl.ds(row0, SLOT), :] = xg[part]
                p_col = jnp.sum(jnp.where(masks[jj], gate_s[b, pl.ds(e + jj, 1), :], 0.0), axis=1, keepdims=True)
                do_s[jj, pl.ds(row0, SLOT), :] = (p_col * gg[part]).astype(BF16)

            @pl.when(b < 2)
            def _():
                for jj in range(GROUP):
                    gg_s[jj, pl.ds(row0, SLOT), :] = gg[jj * SLOT:(jj + 1) * SLOT].astype(BF16)
            return 0
        lax.fori_loop(0, SHARDS, gather, 0)

    def compute(slot, first):
        x_rows = xg_s[slot]
        do_rows = do_s[slot]
        for n in range(2):
            cols = slice(n * 256, (n + 1) * 256)
            z1 = dot_nn(x_rows, w1_ref[0, :, cols])
            z3 = dot_nn(x_rows, w3_ref[0, :, cols])
            da = dot_nt(do_rows, w2_ref[0, cols, :])
            sig = jax.nn.sigmoid(z1)
            silu = z1 * sig
            a_s[:, cols] = (silu * z3).astype(BF16)
            dz1_s[:, cols] = (da * z3 * sig * (1.0 + z1 * (1.0 - sig))).astype(BF16)
            dz3_s[:, cols] = (da * silu).astype(BF16)
        g1 = dot_tn(x_rows, dz1_s[...])
        g3 = dot_tn(x_rows, dz3_s[...])
        g2 = dot_tn(a_s[...], do_rows)
        if first:
            o1_ref[0] = g1
            o3_ref[0] = g3
            o2_ref[0] = g2
        else:
            o1_ref[0] += g1
            o3_ref[0] += g3
            o2_ref[0] += g2

    def own_rows(row0, gg_rows):
        rows = pl.ds(row0, 2 * SLOT)
        o = dot_nn(a_s[rows, :], w2_ref[0])
        q = jnp.sum(o * gg_rows.astype(F32), axis=1, keepdims=True)
        dx = (dot_nt(dz1_s[rows, :], w1_ref[0]) + dot_nt(dz3_s[rows, :], w3_ref[0])).astype(BF16)
        return q, dx

    compute(j, True)
    q, dx = own_rows(0, gg_s[j])
    for b in range(2):
        part = slice(b * SLOT, (b + 1) * SLOT)
        r_s[b, pl.ds(pl.multiple_of(j * SLOT, SLOT), SLOT), :] = dx[part]
        q_ref[b, pl.ds(i, 1), :] = jnp.sum(jnp.where(slot_mask(b, e, SLOT, 0.0), q[part], 0.0), axis=0, keepdims=True)

    @pl.when(j == GROUP - 1)
    def _():
        for b in range(2):
            sel = jnp.concatenate([as_bf16(slot_mask(b, e - (GROUP - 1) + jj, SLOT, 0.0)) for jj in range(GROUP)], axis=0)
            s_ref[b] += dot_tn(sel, r_s[b])

    n_hot = jnp.int32(0)
    for b in range(SHARDS):
        list_s[b] = jnp.int32(0)
    for b in range(SHARDS):
        hit = hot_s[b] == e

        @pl.when(hit)
        def _(b=b, n_hot=n_hot):
            list_s[n_hot] = jnp.int32(b)
        n_hot = n_hot + hit.astype(jnp.int32)

    def hot_chunk(c, _):
        def gather(k, _):
            pos = c * 4 + k
            b = list_s[pos]
            s = shard_of(b)
            live = pos < n_hot
            mask = slot_mask(b, e, HOT, jnp.where(live, float(SLOT), 4096.0))
            sel = as_bf16(mask)
            rows = pl.ds(pl.multiple_of(k * HOT, HOT), HOT)
            xg_s[GROUP, rows, :] = dot_nn(sel, x_ref[s]).astype(BF16)
            gg = dot_nn(sel, g_ref[s])
            p_col = jnp.sum(jnp.where(mask, gate_s[b, pl.ds(e, 1), :], 0.0), axis=1, keepdims=True)
            do_s[GROUP, rows, :] = (p_col * gg).astype(BF16)

            @pl.when(k < 2)
            def _():
                gg_s[GROUP + k] = gg.astype(BF16)
            return 0
        lax.fori_loop(0, 4, gather, 0)
        compute(GROUP, False)

        def own(k, _):
            b = list_s[k]

            @pl.when((c == 0) & (k < n_hot) & (b < 2))
            def _():
                q, dx = own_rows(pl.multiple_of(k * HOT, HOT), gg_s[GROUP + k])
                mask = slot_mask(b, e, HOT, float(SLOT))
                s_ref[b] += dot_tn(as_bf16(mask), dx)
                q_ref[b, pl.ds(i, 1), :] += jnp.sum(jnp.where(mask, q, 0.0), axis=0, keepdims=True)
            return 0
        lax.fori_loop(0, 2, own, 0)
        return 0

    lax.fori_loop(0, lax.div(n_hot + 3, 4), hot_chunk, 0)


def expert_pass(info, x_all, g_all, idx_all, w_router, w_gate, w_up, w_down):
    vmem = pl.BlockSpec(memory_space=pltpu.VMEM)
    up_spec = pl.BlockSpec((1, D, FF), lambda i, info: (i, 0, 0))
    down_spec = pl.BlockSpec((1, FF, D), lambda i, info: (i, 0, 0))
    return pl.pallas_call(
        main_kernel,
        out_shape=(
            jax.ShapeDtypeStruct((E_LOC, D, FF), F32),
            jax.ShapeDtypeStruct((E_LOC, D, FF), F32),
            jax.ShapeDtypeStruct((E_LOC, FF, D), F32),
            jax.ShapeDtypeStruct((2, TOK, D), F32),
            jax.ShapeDtypeStruct((2, E_LOC, TOK), F32),
            jax.ShapeDtypeStruct((2, EXPERTS, TOK), F32),
        ),
        grid_spec=pltpu.PrefetchScalarGridSpec(
            num_scalar_prefetch=1,
            grid=(E_LOC,),
            in_specs=[vmem, vmem, vmem, vmem, up_spec, up_spec, down_spec],
            out_specs=(up_spec, up_spec, down_spec, vmem, vmem, vmem),
            scratch_shapes=[
                pltpu.VMEM((SHARDS, EXPERTS, TOK), F32),
                pltpu.VMEM((SHARDS, EXPERTS, TOK), F32),
                pltpu.SMEM((SHARDS,), jnp.int32),
                pltpu.SMEM((SHARDS,), jnp.int32),
                pltpu.VMEM((GROUP + 1, ROWS, D), BF16),
                pltpu.VMEM((GROUP + 1, ROWS, D), BF16),
                pltpu.VMEM((GROUP + 2, 2 * SLOT, D), BF16),
                pltpu.VMEM((2, GROUP * SLOT, D), BF16),
                pltpu.VMEM((ROWS, FF), BF16),
                pltpu.VMEM((ROWS, FF), BF16),
                pltpu.VMEM((ROWS, FF), BF16),
            ],
        ),
        compiler_params=pltpu.CompilerParams(
            dimension_semantics=("arbitrary",), vmem_limit_bytes=64_000_000),
        cost_estimate=pl.CostEstimate(flops=90_000_000_000, bytes_accessed=170_000_000, transcendentals=8_000_000),
        name="experts",
    )(info, x_all, g_all, idx_all, w_router, w_gate, w_up, w_down)


def solution(mesh):
    tok_spec = P(("dp", "ep"), None)
    exp_spec = P("ep", None, None)

    def device_step(x_loc, route_idx, w_router, w_gate, w_up, w_down, dy_loc):
        core = lax.axis_index("ep")
        dp = lax.axis_index("dp")
        info = jnp.stack([core, dp]).astype(jnp.int32)
        x_all = lax.all_gather(x_loc, ("dp", "ep"))
        g_all = lax.all_gather(dy_loc, ("dp", "ep"))
        idx_all = lax.all_gather(route_idx.T, ("dp", "ep"))
        g1, g3, g2, dx_part, q_part, gates = expert_pass(info, x_all, g_all, idx_all, w_router, w_gate, w_up, w_down)
        swap = [(0, 1), (1, 0)]
        mine = lambda v: lax.dynamic_index_in_dim(v, core, 0, keepdims=False)
        other = lambda v: lax.ppermute(lax.dynamic_index_in_dim(v, 1 - core, 0, keepdims=False), "ep", swap)
        q_mine, q_other = mine(q_part), other(q_part)
        q_all = jnp.where(core == 0, jnp.concatenate([q_mine, q_other]), jnp.concatenate([q_other, q_mine]))
        p_all = mine(gates)
        d_log = (p_all * (q_all - jnp.sum(p_all * q_all, axis=0, keepdims=True))).astype(BF16)
        du = lax.dot_general(d_log, w_router, (((0,), (1,)), ((), ())), preferred_element_type=F32)
        grad_x = (mine(dx_part) + other(dx_part) + du).astype(BF16)
        d_log_all = lax.all_gather(d_log, ("dp", "ep"))
        grad_router = lax.dot_general(x_all, d_log_all, (((0, 1), (0, 2)), ((), ())), preferred_element_type=F32)
        return grad_x, g1, g3, g2, grad_router

    return jax.shard_map(device_step, mesh=mesh, in_specs=(tok_spec, tok_spec, P(), exp_spec, exp_spec, exp_spec, tok_spec), out_specs=(tok_spec, exp_spec, exp_spec, exp_spec, P()), check_vma=False)
```

profile of v0, /device:TPU:0, one launch (start us, length us, event | category | flops | bytes accessed | tf_op | source)
XLA Modules:
  0.0 218.2 jit_solution(13005112621771292303)
XLA Ops:
  7.2 0.0 all-gather.6.cloned.1.call-start
  7.2 0.7 all-gather.6.cloned.1.call-update
  7.9 0.0 all-gather.8.cloned.1.call-start
  7.9 0.7 all-gather.8.cloned.1.call-update
  8.7 1.7 copy.13.wr_ref
  10.3 14.4 %all-gather.2 = s32[64,256]{1,0:T(8,128)} all-gather(s32[8,256]{1,0:T(8,128)} %bitcast.41), channel_id=4, replica_groups=mesh['dp'=4,'ep'=2] {'dp','ep'}, dimensions={0}, use_global_device_ids=true | all-gather | bytes 73728 | tf_op jit(solution)/shard_map/all_gather | solution.py:255
  24.8 0.6 pad_add_fusion.info
  25.4 18.5 %all-gather.6.cloned.1.call-done = bf16[2048,1024]{1,0:T(8,128)(2,1)} async-done(((bf16[256,1024]{1,0:T(8,128)(2,1)}), bf16[2048,1024]{1,0:T(8,128)(2,1)}) %all-gather.6.cloned.1.call-update) | async-done | bytes 4194320 | tf_op jit(solution)/shard_map/all_gather | solution.py:253
  43.9 32.6 %all-gather.8.cloned.1.call-done = bf16[2048,1024]{1,0:T(8,128)(2,1)} async-done(((bf16[256,1024]{1,0:T(8,128)(2,1)}), bf16[2048,1024]{1,0:T(8,128)(2,1)}) %all-gather.8.cloned.1.call-update) | async-done | bytes 4194320 | tf_op jit(solution)/shard_map/all_gather | solution.py:254
  76.5 99.7 %experts.1 = (f32[16,1024,512]{2,1,0:T(8,128)}, f32[16,1024,512]{2,1,0:T(8,128)}, f32[16,512,1024]{2,1,0:T(8,128)}, f32[2,256,1024]{2,1,0:T(8,128)}, f32[2,16,256]{2,1,0:T(8,128)}, /*index=5*/f32[2,32,256]{2,1,0:T(8,128)}) custom-call(s32[2]{0:T(128)} %pad_add_fusion.info, bf16[8,256,1024]{2,1,0:T(8,128)(2,1)} %bitcast.35, bf16[8,256,1024]{2,1,0:T(8,128)(2,1)} %bitcast.42, ...), custom_call_target="tpu_custom_call" | custom-call | flops 89999998976 | bytes 170000000 | tf_op jit(solution)/shard_map/experts/pallas_call | solution.py:209
  176.2 0.0 copy-start
  176.2 0.0 copy-start.1
  176.2 0.0 copy-start.2
  176.2 1.5 dynamic-slice_bitcast_fusion
  177.7 12.7 %collective-permute-start = (f32[256,1024]{1,0:T(8,128)S(1)}, f32[256,1024]{1,0:T(8,128)}, u32[]{:S(2)}, u32[]{:S(2)}) collective-permute-start(f32[256,1024]{1,0:T(8,128)S(1)} %dynamic-slice_bitcast_fusion), channel_id=1, source_target_pairs={{0,1},{1,0},{2,3},{3,2},{4,5},{5,4},{6,7},{7,6}} | collective-permute-start | bytes 3145736 | tf_op jit(solution)/shard_map/ppermute | solution.py:259
  190.3 0.7 dynamic-slice_bitcast_fusion.1
  191.1 0.0 collective-permute-start.1
  191.1 1.5 collective-permute-done.1
  192.7 0.8 fusion.5
  193.4 0.8 fusion.4
  194.2 11.1 %all_gather.28 = bf16[8,32,256]{2,1,0:T(8,128)(2,1)S(1)} all-gather(bf16[1,32,256]{2,1,0:T(8,128)(2,1)S(1)} %fusion.4), channel_id=1, replica_groups=mesh['dp'=4,'ep'=2] {'dp','ep'}, dimensions={0}, use_global_device_ids=true | all-gather | bytes 147456 | tf_op jit(solution)/shard_map/all_gather | solution.py:266
  205.3 3.7 %convolution_bitcast_fusion = f32[1024,32]{0,1:T(8,128)} fusion(bf16[8,32,256]{2,1,0:T(8,128)(2,1)S(1)} %all_gather.28, bf16[8,256,1024]{2,1,0:T(8,128)(2,1)} %bitcast.36), kind=kOutput, calls=%fused_computation | convolution fusion | flops 134217728 | bytes 4456448 | tf_op jit(solution)/shard_map/dot_general | solution.py:267
  209.0 0.0 collective-permute-done
  209.0 0.0 copy-done
  209.0 0.0 copy-done.1
  209.0 0.0 copy-done.2
  209.0 2.3 %fusion.1 = bf16[256,1024]{1,0:T(8,128)(2,1)} fusion(f32[256,1024]{1,0:T(8,128)} %collective-permute-done, f32[2,256,1024]{2,1,0:T(8,128)S(1)} %copy-done, s32[]{:T(128)S(6)} %select_n.31, bf16[1024,32]{0,1:T(8,128)(2,1)S(1)} %copy-done.1, f32[2,32,256]{2,1,0:T(8,128)S(1)} %copy-done.2, f32[16,256]{1,0:T(8,128)S(1)} %bitcast.38, ...), kind=kOutput, calls=%fused_computation.3 | convolution fusion | flops 17612800 | bytes 2755072 | tf_op jit(solution)/shard_map/dot_general | solution.py:264
Async XLA Ops:
  7.2 36.7 %all-gather.6.cloned.1.call-start = ((), (), s32[]{:S(2)}) async-start(), calls=%async_computation | async-start | bytes 4718592 | tf_op jit(solution)/shard_map/all_gather | solution.py:253
  7.9 68.6 %all-gather.8.cloned.1.call-start = ((), (), s32[]{:S(2)}) async-start(), calls=%async_computation.1 | async-start | bytes 4718592 | tf_op jit(solution)/shard_map/all_gather | solution.py:254
  176.2 32.8 %copy-start = (f32[2,256,1024]{2,1,0:T(8,128)S(1)}, f32[2,256,1024]{2,1,0:T(8,128)}, u32[]{:S(2)}) copy-start(f32[2,256,1024]{2,1,0:T(8,128)} %get-tuple-element.11) | copy-start | bytes 6291460
  176.2 32.8 %copy-start.1 = (bf16[1024,32]{0,1:T(8,128)(2,1)S(1)}, bf16[1024,32]{0,1:T(8,128)(2,1)}, u32[]{:S(2)}) copy-start(bf16[1024,32]{0,1:T(8,128)(2,1)} %param.9) | copy-start | bytes 196612
  176.2 32.8 %copy-start.2 = (f32[2,32,256]{2,1,0:T(8,128)S(1)}, f32[2,32,256]{2,1,0:T(8,128)}, u32[]{:S(2)}) copy-start(f32[2,32,256]{2,1,0:T(8,128)} %get-tuple-element.12) | copy-start | bytes 196612
  177.7 31.3 %collective-permute-start = (f32[256,1024]{1,0:T(8,128)S(1)}, f32[256,1024]{1,0:T(8,128)}, u32[]{:S(2)}, u32[]{:S(2)}) collective-permute-start(f32[256,1024]{1,0:T(8,128)S(1)} %dynamic-slice_bitcast_fusion), channel_id=1, source_target_pairs={{0,1},{1,0},{2,3},{3,2},{4,5},{5,4},{6,7},{7,6}} | collective-permute-start | bytes 3145736 | tf_op jit(solution)/shard_map/ppermute | solution.py:259
  191.1 1.6 collective-permute-start.1
Sparse Core Ops, SparseCore 0:
  9.8 34.0 all-gather.5
  45.7 30.7 all-gather.7
where the time goes:
time: 219 us; the launch traced here: 218 us
  Pallas kernels  99.7 us (46%)
  waiting for transfers between devices  54 us (25%)
  blocking collectives  25.5 us (12%)
  between operations  14.1 us (6%)
  starting transfers between devices  12.8 us (6%)
  matrix products  6.02 us (3%)
  local copies, waits for them, and re-layouts  3.89 us (2%)
    pallas_call x1, Pallas kernels, expert_pass(): pl.pallas_call(main_kernel, out_shape=(jax.ShapeDtypeStruct((E_LOC, D, FF...  99.7 us
    all_gather x1, waiting for transfers between devices, device_step(): g_all = lax.all_gather(dy_loc, ('dp', 'ep'))  32.6 us
    all_gather x1, waiting for transfers between devices, device_step(): x_all = lax.all_gather(x_loc, ('dp', 'ep'))  18.5 us
    all_gather x1, blocking collectives, device_step(): idx_all = lax.all_gather(route_idx.T, ('dp', 'ep'))  14.4 us
    ppermute x2, starting transfers between devices, device_step(): lax.ppermute(lax.dynamic_index_in_dim(v, 1 - core, 0, keepdims=False), 'e...  12.7 us
    all_gather x1, blocking collectives, device_step(): d_log_all = lax.all_gather(d_log, ('dp', 'ep'))  11.1 us
  transfers between devices with their start and end apart: 4, of which 3 were waited for; matrix products, arithmetic and copies ran while one was open for 4% of the time, Pallas kernels for 0%

commit v1 on v0

--- a/solution.py
+++ b/solution.py
@@ -1,5 +1,3 @@
-import functools
-
 import jax
 import jax.numpy as jnp
 from jax import lax
@@ -21,6 +19,7 @@
 CAP = 192
 F32 = jnp.float32
 BF16 = jnp.bfloat16
+MESH = pl.DeviceIdType.MESH
 
 
 def dot_nn(a, b):
@@ -56,13 +55,8 @@
                 o1_ref, o3_ref, o2_ref, s_ref, q_ref, gate_ref,
                 code_s, gate_s, hot_s, list_s, xg_s, do_s, gg_s, r_s, a_s, dz1_s, dz3_s):
     i = pl.program_id(0)
-    core = info[0]
-    dp = info[1]
-    e = core * E_LOC + i
+    e = info[0] * E_LOC + i
     j = lax.rem(i, GROUP)
-
-    def shard_of(b):
-        return lax.rem(2 * dp + b, SHARDS)
 
     def slot_mask(b, ex, rows, base):
         row = code_s[b, pl.ds(ex, 1), :] - base
@@ -75,8 +69,7 @@
     @pl.when(i == 0)
     def _():
         def prep(b, _):
-            s = shard_of(b)
-            code, gates, count = route_tables(x_ref[s], idx_ref[s], wr_ref[...])
+            code, gates, count = route_tables(x_ref[b], idx_ref[b], wr_ref[...])
             code_s[b] = code
             gate_s[b] = gates
             e_col = lax.broadcasted_iota(jnp.int32, (EXPERTS, 1), 0).astype(F32)
@@ -90,11 +83,10 @@
     @pl.when(j == 0)
     def _():
         def gather(b, _):
-            s = shard_of(b)
             masks = [slot_mask(b, e + jj, SLOT, 0.0) for jj in range(GROUP)]
             sel = jnp.concatenate([as_bf16(m) for m in masks], axis=0)
-            xg = dot_nn(sel, x_ref[s]).astype(BF16)
-            gg = dot_nn(sel, g_ref[s])
+            xg = dot_nn(sel, x_ref[b]).astype(BF16)
+            gg = dot_nn(sel, g_ref[b])
             row0 = pl.multiple_of(b * SLOT, SLOT)
             for jj in range(GROUP):
                 part = slice(jj * SLOT, (jj + 1) * SLOT)
@@ -169,13 +161,12 @@
         def gather(k, _):
             pos = c * 4 + k
             b = list_s[pos]
-            s = shard_of(b)
             live = pos < n_hot
             mask = slot_mask(b, e, HOT, jnp.where(live, float(SLOT), 4096.0))
             sel = as_bf16(mask)
             rows = pl.ds(pl.multiple_of(k * HOT, HOT), HOT)
-            xg_s[GROUP, rows, :] = dot_nn(sel, x_ref[s]).astype(BF16)
-            gg = dot_nn(sel, g_ref[s])
+            xg_s[GROUP, rows, :] = dot_nn(sel, x_ref[b]).astype(BF16)
+            gg = dot_nn(sel, g_ref[b])
             p_col = jnp.sum(jnp.where(mask, gate_s[b, pl.ds(e, 1), :], 0.0), axis=1, keepdims=True)
             do_s[GROUP, rows, :] = (p_col * gg).astype(BF16)
 
@@ -242,29 +233,158 @@
     )(info, x_all, g_all, idx_all, w_router, w_gate, w_up, w_down)
 
 
+def peer(step):
+    chip = lax.axis_index("dp")
+    core = lax.axis_index("ep")
+    x_bit, y_bit = lax.rem(chip, 2), lax.div(chip, 2)
+    if step & 2:
+        x_bit = 1 - x_bit
+    if step & 4:
+        y_bit = 1 - y_bit
+    if step & 1:
+        core = 1 - core
+    return {"dp": 2 * y_bit + x_bit, "ep": core}
+
+
+def greet_all():
+    barrier = pltpu.get_barrier_semaphore()
+    for step in range(1, SHARDS):
+        pl.semaphore_signal(barrier, inc=1, device_id=peer(step), device_id_type=MESH)
+    pl.semaphore_wait(barrier, SHARDS - 1)
+
+
+def share_kernel(x_ref, g_ref, idx_ref, x_all, g_all, idx_all, send, recv, local):
+    def copy(ref, into, sem, slot, step):
+        return pltpu.make_async_remote_copy(
+            src_ref=ref, dst_ref=into.at[slot], send_sem=send.at[sem], recv_sem=recv.at[sem],
+            device_id=peer(step), device_id_type=MESH)
+
+    own = [pltpu.make_async_copy(ref, into.at[0], local.at[n])
+           for n, (ref, into) in enumerate(((x_ref, x_all), (g_ref, g_all), (idx_ref, idx_all)))]
+    for c in own:
+        c.start()
+    greet_all()
+    ids = [copy(idx_ref, idx_all, 14 + k - 1, k, k) for k in range(1, SHARDS)]
+    for c in ids:
+        c.start()
+    x1, g1 = copy(x_ref, x_all, 0, 1, 1), copy(g_ref, g_all, 7, 1, 1)
+    x2, g2 = copy(x_ref, x_all, 1, 2, 2), copy(g_ref, g_all, 8, 2, 2)
+    g4, x4 = copy(g_ref, g_all, 10, 4, 4), copy(x_ref, x_all, 3, 4, 4)
+    x6, g6 = copy(x_all.at[2], x_all, 5, 6, 4), copy(g_all.at[4], g_all, 12, 6, 2)
+    x3, g3 = copy(x_all.at[2], x_all, 2, 3, 1), copy(g_all.at[2], g_all, 9, 3, 1)
+    x5, g5 = copy(x_all.at[4], x_all, 4, 5, 1), copy(g_all.at[4], g_all, 11, 5, 1)
+    x7, g7 = copy(x_all.at[6], x_all, 6, 7, 1), copy(g_all.at[6], g_all, 13, 7, 1)
+    for c in (x1, g1, x2, g4, g2, x4):
+        c.start()
+    x2.wait_recv()
+    x6.start()
+    x3.start()
+    g4.wait_recv()
+    g6.start()
+    g5.start()
+    g2.wait_recv()
+    g3.start()
+    x4.wait_recv()
+    x5.start()
+    x6.wait_recv()
+    x7.start()
+    g6.wait_recv()
+    g7.start()
+    for c in (x1, g1, x3, g3, x5, g5, x7, g7, *ids):
+        c.wait_recv()
+    for c in (x1, g1, x2, g2, g4, x4, x6, g6, x3, g3, x5, g5, x7, g7, *ids):
+        c.wait_send()
+    for c in own:
+        c.wait()
+
+
+def share_tokens(x_loc, dy_loc, idx_t):
+    vmem = pl.BlockSpec(memory_space=pltpu.VMEM)
+    hbm = pl.BlockSpec(memory_space=pl.ANY)
+    return pl.pallas_call(
+        share_kernel,
+        out_shape=(
+            jax.ShapeDtypeStruct((SHARDS, TOK, D), BF16),
+            jax.ShapeDtypeStruct((SHARDS, TOK, D), BF16),
+            jax.ShapeDtypeStruct((SHARDS, TOP, TOK), jnp.int32),
+        ),
+        in_specs=[vmem, vmem, vmem],
+        out_specs=(hbm, hbm, hbm),
+        scratch_shapes=[
+            pltpu.SemaphoreType.DMA((21,)),
+            pltpu.SemaphoreType.DMA((21,)),
+            pltpu.SemaphoreType.DMA((3,)),
+        ],
+        compiler_params=pltpu.CompilerParams(collective_id=0, has_side_effects=True),
+        name="share",
+    )(x_loc, dy_loc, idx_t)
+
+
+def tail_kernel(s_ref, q_ref, gate_ref, x_all, wr_ref, gx_ref, gr_ref, s_got, q_got, dl_all, send, recv):
+    core = lax.axis_index("ep")
+
+    def copy(ref, into, sem, step):
+        return pltpu.make_async_remote_copy(
+            src_ref=ref, dst_ref=into, send_sem=send.at[sem], recv_sem=recv.at[sem],
+            device_id=peer(step), device_id_type=MESH)
+
+    greet_all()
+    q_copy = copy(q_ref.at[1], q_got, 0, 1)
+    s_copy = copy(s_ref.at[1], s_got, 1, 1)
+    q_copy.start()
+    s_copy.start()
+    q_copy.wait_recv()
+    low = jnp.concatenate([q_ref[0], q_got[...]], axis=0)
+    high = jnp.concatenate([q_got[...], q_ref[0]], axis=0)
+    q = jnp.where(core == 0, low, high)
+    p = gate_ref[0]
+    d_log = (p * (q - jnp.sum(p * q, axis=0, keepdims=True))).astype(BF16)
+    dl_all[0] = d_log
+    copies = [copy(dl_all.at[0], dl_all.at[k], 1 + k, k) for k in range(1, SHARDS)]
+    for c in copies:
+        c.start()
+    du = lax.dot_general(d_log, wr_ref[...], (((0,), (1,)), ((), ())), preferred_element_type=F32)
+    s_copy.wait_recv()
+    gx_ref[...] = (s_ref[0] + s_got[...] + du).astype(BF16)
+    total = lax.dot_general(x_all[0], d_log, (((0,), (1,)), ((), ())), preferred_element_type=F32)
+    for k in range(1, SHARDS):
+        copies[k - 1].wait_recv()
+        total += lax.dot_general(x_all[k], dl_all[k], (((0,), (1,)), ((), ())), preferred_element_type=F32)
+    gr_ref[...] = total
+    q_copy.wait_send()
+    s_copy.wait_send()
+    for c in copies:
+        c.wait_send()
+
+
+def tail(dx_part, q_part, gates, x_all, w_router):
+    vmem = pl.BlockSpec(memory_space=pltpu.VMEM)
+    return pl.pallas_call(
+        tail_kernel,
+        out_shape=(jax.ShapeDtypeStruct((TOK, D), BF16), jax.ShapeDtypeStruct((D, EXPERTS), F32)),
+        in_specs=[vmem] * 5,
+        out_specs=(vmem, vmem),
+        scratch_shapes=[
+            pltpu.VMEM((TOK, D), F32),
+            pltpu.VMEM((E_LOC, TOK), F32),
+            pltpu.VMEM((SHARDS, EXPERTS, TOK), BF16),
+            pltpu.SemaphoreType.DMA((9,)),
+            pltpu.SemaphoreType.DMA((9,)),
+        ],
+        compiler_params=pltpu.CompilerParams(collective_id=1, has_side_effects=True, vmem_limit_bytes=32_000_000),
+        name="tail",
+    )(dx_part, q_part, gates, x_all, w_router)
+
+
 def solution(mesh):
     tok_spec = P(("dp", "ep"), None)
     exp_spec = P("ep", None, None)
 
     def device_step(x_loc, route_idx, w_router, w_gate, w_up, w_down, dy_loc):
-        core = lax.axis_index("ep")
-        dp = lax.axis_index("dp")
-        info = jnp.stack([core, dp]).astype(jnp.int32)
-        x_all = lax.all_gather(x_loc, ("dp", "ep"))
-        g_all = lax.all_gather(dy_loc, ("dp", "ep"))
-        idx_all = lax.all_gather(route_idx.T, ("dp", "ep"))
+        info = lax.axis_index("ep").astype(jnp.int32).reshape(1)
+        x_all, g_all, idx_all = share_tokens(x_loc, dy_loc, route_idx.T)
         g1, g3, g2, dx_part, q_part, gates = expert_pass(info, x_all, g_all, idx_all, w_router, w_gate, w_up, w_down)
-        swap = [(0, 1), (1, 0)]
-        mine = lambda v: lax.dynamic_index_in_dim(v, core, 0, keepdims=False)
-        other = lambda v: lax.ppermute(lax.dynamic_index_in_dim(v, 1 - core, 0, keepdims=False), "ep", swap)
-        q_mine, q_other = mine(q_part), other(q_part)
-        q_all = jnp.where(core == 0, jnp.concatenate([q_mine, q_other]), jnp.concatenate([q_other, q_mine]))
-        p_all = mine(gates)
-        d_log = (p_all * (q_all - jnp.sum(p_all * q_all, axis=0, keepdims=True))).astype(BF16)
-        du = lax.dot_general(d_log, w_router, (((0,), (1,)), ((), ())), preferred_element_type=F32)
-        grad_x = (mine(dx_part) + other(dx_part) + du).astype(BF16)
-        d_log_all = lax.all_gather(d_log, ("dp", "ep"))
-        grad_router = lax.dot_general(x_all, d_log_all, (((0, 1), (0, 2)), ((), ())), preferred_element_type=F32)
+        grad_x, grad_router = tail(dx_part, q_part, gates, x_all, w_router)
         return grad_x, g1, g3, g2, grad_router
 
     return jax.shard_map(device_step, mesh=mesh, in_specs=(tok_spec, tok_spec, P(), exp_spec, exp_spec, exp_spec, tok_spec), out_specs=(tok_spec, exp_spec, exp_spec, exp_spec, P()), check_vma=False)

time: 219 us -> 173 us (0.79)
  Pallas kernels: 99.7 us -> 163 us
  waiting for transfers between devices: 54 us -> 0 us
  blocking collectives: 25.5 us -> 0 us
  between operations: 14.1 us -> 0.69 us
  starting transfers between devices: 12.8 us -> 0 us
  matrix products: 6.02 us -> 0 us
  local copies, waits for them, and re-layouts: 3.89 us -> 8.68 us
    pallas_call x0 -> x2, Pallas kernels: none -> 52.1 us  [the longest x1 44.1 us: share_tokens(): pl.pallas_call(share_kernel, out_shape=(jax.ShapeDtypeStruct((SHARDS, TOK...]
    all_gather x2 -> x0, waiting for transfers between devices: 51.1 us -> none  [the longest x1 32.6 us: device_step(): g_all = lax.all_gather(dy_loc, ('dp', 'ep'))]
    all_gather x2 -> x0, blocking collectives: 25.5 us -> none  [the longest x1 14.4 us: device_step(): idx_all = lax.all_gather(route_idx.T, ('dp', 'ep'))]
    ppermute x2 -> x0, starting transfers between devices: 12.7 us -> none  [device_step(): lax.ppermute(lax.dynamic_index_in_dim(v, 1 - core, 0, keepdims=False), 'e...]
    pallas_call x1, Pallas kernels: 99.7 us -> 111 us  [expert_pass(): pl.pallas_call(main_kernel, out_shape=(jax.ShapeDtypeStruct((E_LOC, D, FF...]
    unnamed x7 -> x13, local copies, waits for them, and re-layouts: 1.7 us -> 8.68 us
    dot_general x2 -> x0, matrix products: 6.02 us -> none  [the longest x1 3.67 us: device_step(): lax.dot_general(x_all, d_log_all, (((0, 1), (0, 2)), ((), ())), preferred...]
  transfers between devices with their start and end apart: 4 -> 0, of which waited for: 3 -> 0; matrix products, arithmetic and copies ran while one was open for 4% -> 0% of each run, Pallas kernels for 0% -> 0%
where the time goes in v1:
time: 173 us
  Pallas kernels  163 us (94%)
  local copies, waits for them, and re-layouts  8.68 us (5%)
    pallas_call x1, Pallas kernels, expert_pass(): pl.pallas_call(main_kernel, out_shape=(jax.ShapeDtypeStruct((E_LOC, D, FF...  111 us
    pallas_call x1, Pallas kernels, share_tokens(): pl.pallas_call(share_kernel, out_shape=(jax.ShapeDtypeStruct((SHARDS, TOK...  44.1 us
    unnamed x13, local copies, waits for them, and re-layouts  8.68 us
    pallas_call x1, Pallas kernels, tail(): pl.pallas_call(tail_kernel, out_shape=(jax.ShapeDtypeStruct((TOK, D), BF1...  8 us

profile of v1, /device:TPU:0, one launch (start us, length us, event | category | flops | bytes accessed | tf_op | source)
XLA Modules:
  0.0 172.8 jit_solution(12325643514966491055)
XLA Ops:
  0.6 1.7 copy.12.wr_ref
  2.3 44.1 %share.1 = (bf16[8,256,1024]{2,1,0:T(8,128)(2,1)}, bf16[8,256,1024]{2,1,0:T(8,128)(2,1)}, s32[8,8,256]{2,1,0:T(8,128)}) custom-call(bf16[256,1024]{1,0:T(8,128)(2,1)} %x_ref.1, bf16[256,1024]{1,0:T(8,128)(2,1)} %g_ref.1, s32[8,256]{1,0:T(8,128)} %bitcast.2), custom_call_target="tpu_custom_call" | custom-call | tf_op jit(solution)/shard_map/share/pallas_call | solution.py:304
  46.5 0.0 copy-start.2
  46.5 111.3 %experts.1 = (f32[16,1024,512]{2,1,0:T(8,128)}, f32[16,1024,512]{2,1,0:T(8,128)}, f32[16,512,1024]{2,1,0:T(8,128)}, f32[2,256,1024]{2,1,0:T(8,128)}, f32[2,16,256]{2,1,0:T(8,128)}, /*index=5*/f32[2,32,256]{2,1,0:T(8,128)}) custom-call(s32[1]{0:T(128)} %bitcast.info, bf16[8,256,1024]{2,1,0:T(8,128)(2,1)} %get-tuple-element.16.x_ref.x_all, ...), custom_call_target="tpu_custom_call" | custom-call | flops 89999998976 | bytes 170000000 | tf_op jit(solution)/shard_map/experts/pallas_call | solution.py:200
  157.8 0.0 copy-done.2
  157.8 0.0 copy-start
  157.8 2.2 %copy-done = bf16[8,256,1024]{2,1,0:T(8,128)(2,1)S(1)} copy-done((bf16[8,256,1024]{2,1,0:T(8,128)(2,1)S(1)}, bf16[8,256,1024]{2,1,0:T(8,128)(2,1)}, u32[]{:S(2)}) %copy-start) | copy-done | bytes 4194328
  160.0 0.0 copy-start.1
  160.0 1.6 copy-done.1
  161.6 0.0 copy-start.3
  161.6 0.8 copy-done.3
  162.4 0.0 copy-start.4
  162.4 0.8 copy-done.4
  163.2 8.0 %tail.1 = (bf16[256,1024]{1,0:T(8,128)(2,1)S(1)}, f32[1024,32]{1,0:T(8,128)S(1)}) custom-call(f32[2,256,1024]{2,1,0:T(8,128)S(1)} %copy-done.1, f32[2,16,256]{2,1,0:T(8,128)S(1)} %copy-done.4, f32[2,32,256]{2,1,0:T(8,128)S(1)} %copy-done.3, bf16[8,256,1024]{2,1,0:T(8,128)(2,1)S(1)} %copy-done, bf16[1024,32]{1,0:T(8,128)(2,1)S(1)} %copy-done.2), custom_call_target="tpu_custom_call" | custom-call | tf_op jit(solution)/shard_map/tail/pallas_call | solution.py:362
  171.2 0.8 copy.14
  172.0 0.8 copy.16
Async XLA Ops:
  46.5 111.3 %copy-start.2 = (bf16[1024,32]{1,0:T(8,128)(2,1)S(1)}, bf16[1024,32]{1,0:T(8,128)(2,1)}, u32[]{:S(2)}) copy-start(bf16[1024,32]{1,0:T(8,128)(2,1)} %copy.12.wr_ref) | copy-start | bytes 196612
  157.8 2.2 %copy-start = (bf16[8,256,1024]{2,1,0:T(8,128)(2,1)S(1)}, bf16[8,256,1024]{2,1,0:T(8,128)(2,1)}, u32[]{:S(2)}) copy-start(bf16[8,256,1024]{2,1,0:T(8,128)(2,1)} %get-tuple-element.16.x_ref.x_all) | copy-start | bytes 12582916
  160.0 1.6 copy-start.1
  161.6 0.8 copy-start.3
  162.4 0.8 copy-start.4

commit v2 on v1

v2 whole, which is shorter than its diff:
```python
import jax
import jax.numpy as jnp
from jax import lax
from jax.experimental import pallas as pl
from jax.experimental.pallas import tpu as pltpu
from jax.sharding import PartitionSpec as P

D = 1024
FF = 512
EXPERTS = 32
TOP = 8
TOK = 256
SHARDS = 8
E_LOC = 16
SLOT = 64
GROUP = 4
ROWS = SHARDS * SLOT
HOT = 128
OWN = 2 * SLOT
FORWARD = (5, 9, 14)
VMEM_ALL = 67_000_000
CAP = 192
F32 = jnp.float32
BF16 = jnp.bfloat16
MESH = pl.DeviceIdType.MESH


def dot_nn(a, b):
    return lax.dot_general(a, b, (((1,), (0,)), ((), ())), preferred_element_type=F32)


def dot_nt(a, b):
    return lax.dot_general(a, b, (((1,), (1,)), ((), ())), preferred_element_type=F32)


def dot_tn(a, b):
    return lax.dot_general(a, b, (((0,), (0,)), ((), ())), preferred_element_type=F32)


def route_tables(x_s, idx_t, w_router_t):
    logits = dot_nt(w_router_t, x_s)
    e_iota = lax.broadcasted_iota(jnp.int32, (EXPERTS, TOK), 0)
    mask = e_iota == idx_t[0:1, :]
    for k in range(1, TOP):
        mask = mask | (e_iota == idx_t[k:k + 1, :])
    top = jnp.max(jnp.where(mask, logits, -jnp.inf), axis=0, keepdims=True)
    ex = jnp.where(mask, jnp.exp(jnp.where(mask, logits - top, 0.0)), 0.0)
    gates = ex / jnp.sum(ex, axis=0, keepdims=True)
    mask_f = jnp.where(mask, 1.0, 0.0)
    before = lax.broadcasted_iota(jnp.int32, (TOK, TOK), 0) < lax.broadcasted_iota(jnp.int32, (TOK, TOK), 1)
    rank = dot_nn(mask_f.astype(BF16), jnp.where(before, 1.0, 0.0).astype(BF16))
    code = jnp.where(mask, rank, -1.0)
    count = jnp.sum(mask_f, axis=1, keepdims=True)
    return code, gates, count


def slot_mask(code_row, rows, base):
    r_iota = lax.broadcasted_iota(jnp.int32, (rows, TOK), 0).astype(F32)
    return code_row - base == r_iota


def as_bf16(mask):
    return jnp.where(mask, 1.0, 0.0).astype(BF16)


def swiglu_grads(z1, z3, da):
    sig = jax.nn.sigmoid(z1)
    silu = z1 * sig
    act = (silu * z3).astype(BF16)
    dz1 = (da * z3 * sig * (1.0 + z1 * (1.0 - sig))).astype(BF16)
    dz3 = (da * silu).astype(BF16)
    return act, dz1, dz3


def own_grads(act, dz1, dz3, gg, w1, w3, w2):
    o = dot_nn(act, w2)
    q = jnp.sum(o * gg.astype(F32), axis=1, keepdims=True)
    dx = (dot_nt(dz1, w1) + dot_nt(dz3, w3)).astype(BF16)
    return q, dx


def main_kernel(info, x_hbm, g_hbm, idx_ref, wr_ref, s_hbm, q_in, own_x, own_do, own_a, own_dz1, own_dz3,
                w1_ref, w3_ref, w2_ref, o1_ref, o3_ref, o2_ref, s_ref, q_ref,
                x_s, g_s, code_s, gate_s, hot_s, list_s, xg_s, do_s, xh_s, dh_s, gg_s, a_s, dz1_s, dz3_s, sem):
    i = pl.program_id(0)
    e = info[0] * E_LOC + i
    j = lax.rem(i, GROUP)
    buf = lax.rem(lax.div(i, GROUP), 2)

    def load(ref, into, b, n):
        return pltpu.make_async_copy(ref.at[b], into.at[b], sem.at[n, b])

    s_load = pltpu.make_async_copy(s_hbm, s_ref, sem.at[2, 0])

    def select(b, ex, rows, base):
        return slot_mask(code_s[b, pl.ds(ex, 1), :], rows, base)

    def gather(b, first, into):
        masks = [select(b, first + jj, SLOT, 0.0) for jj in range(GROUP)]
        sel = jnp.concatenate([as_bf16(m) for m in masks], axis=0)
        xg = dot_nn(sel, x_s[b]).astype(BF16)
        gg = dot_nn(sel, g_s[b])
        row0 = pl.multiple_of(b * SLOT, SLOT)
        for jj in range(GROUP):
            part = slice(jj * SLOT, (jj + 1) * SLOT)
            xg_s[into, jj, pl.ds(row0, SLOT), :] = xg[part]
            p_col = jnp.sum(jnp.where(masks[jj], gate_s[b, pl.ds(first + jj, 1), :], 0.0), axis=1, keepdims=True)
            do_s[into, jj, pl.ds(row0, SLOT), :] = (p_col * gg[part]).astype(BF16)

    @pl.when(i == 0)
    def _():
        for b in range(SHARDS):
            load(x_hbm, x_s, b, 0).start()
            load(g_hbm, g_s, b, 1).start()
        s_load.start()

        def prep(b, _):
            load(x_hbm, x_s, b, 0).wait()
            code, gates, count = route_tables(x_s[b], idx_ref[b], wr_ref[...])
            code_s[b] = code
            gate_s[b] = gates
            e_col = lax.broadcasted_iota(jnp.int32, (EXPERTS, 1), 0).astype(F32)
            hot_s[b] = jnp.max(jnp.where(count > SLOT, e_col, -1.0)).astype(jnp.int32)
            load(g_hbm, g_s, b, 1).wait()
            return 0
        lax.fori_loop(0, SHARDS, prep, 0)
        q_ref[...] = q_in[...]

        def first_gather(b, _):
            gather(b, e, 0)
            return 0
        lax.fori_loop(2, SHARDS, first_gather, 0)
        s_load.wait()

    @pl.when((i < E_LOC - GROUP) & (j < 3))
    def _():
        for k in range(2):
            gather(2 + 2 * j + k, e - j + GROUP, 1 - buf)

    def compute(x_at, do_at, first):
        skip = OWN if first else 0
        rest = slice(skip, ROWS)
        for n in range(2):
            cols = slice(n * 256, (n + 1) * 256)
            z1 = dot_nn(x_at[rest, :], w1_ref[0, :, cols])
            z3 = dot_nn(x_at[rest, :], w3_ref[0, :, cols])
            da = dot_nt(do_at[rest, :], w2_ref[0, cols, :])
            act, dz1, dz3 = swiglu_grads(z1, z3, da)
            a_s[rest, cols] = act
            dz1_s[rest, cols] = dz1
            dz3_s[rest, cols] = dz3
        g1 = dot_tn(x_at[...], dz1_s[...])
        g3 = dot_tn(x_at[...], dz3_s[...])
        g2 = dot_tn(a_s[...], do_at[...])
        if first:
            o1_ref[0] = g1
            o3_ref[0] = g3
            o2_ref[0] = g2
        else:
            o1_ref[0] += g1
            o3_ref[0] += g3
            o2_ref[0] += g2

    xg_s[buf, j, :OWN, :] = own_x[0]
    do_s[buf, j, :OWN, :] = own_do[0]
    a_s[:OWN, :] = own_a[0]
    dz1_s[:OWN, :] = own_dz1[0]
    dz3_s[:OWN, :] = own_dz3[0]
    compute(xg_s.at[buf, j], do_s.at[buf, j], True)

    n_hot = jnp.int32(0)
    for b in range(SHARDS):
        list_s[b] = jnp.int32(0)
    for b in range(SHARDS):
        hit = hot_s[b] == e

        @pl.when(hit)
        def _(b=b, n_hot=n_hot):
            list_s[n_hot] = jnp.int32(b)
        n_hot = n_hot + hit.astype(jnp.int32)

    def hot_chunk(c, _):
        def hot_gather(k, _):
            pos = c * 4 + k
            b = list_s[pos]
            live = pos < n_hot
            mask = select(b, e, HOT, jnp.where(live, float(SLOT), 4096.0))
            sel = as_bf16(mask)
            rows = pl.ds(pl.multiple_of(k * HOT, HOT), HOT)
            xh_s[rows, :] = dot_nn(sel, x_s[b]).astype(BF16)
            gg = dot_nn(sel, g_s[b])
            p_col = jnp.sum(jnp.where(mask, gate_s[b, pl.ds(e, 1), :], 0.0), axis=1, keepdims=True)
            dh_s[rows, :] = (p_col * gg).astype(BF16)

            @pl.when(k < 2)
            def _():
                gg_s[rows, :] = gg.astype(BF16)
            return 0
        lax.fori_loop(0, 4, hot_gather, 0)
        compute(xh_s, dh_s, False)

        @pl.when((c == 0) & (list_s[0] < 2))
        def _():
            rows = slice(0, 2 * HOT)
            q, dx = own_grads(a_s[rows, :], dz1_s[rows, :], dz3_s[rows, :], gg_s[...], w1_ref[0], w3_ref[0], w2_ref[0])
            for k in range(2):
                b = list_s[k]

                @pl.when((k < n_hot) & (b < 2))
                def _(k=k, b=b):
                    part = slice(k * HOT, (k + 1) * HOT)
                    mask = select(b, e, HOT, float(SLOT))
                    s_ref[b] += dot_tn(as_bf16(mask), dx[part])
                    q_ref[b, pl.ds(i, 1), :] += jnp.sum(jnp.where(mask, q[part], 0.0), axis=0, keepdims=True)
        return 0

    lax.fori_loop(0, lax.div(n_hot + 3, 4), hot_chunk, 0)


def expert_pass(info, x_all, g_all, idx_all, w_router_t, s_part, q_part, own, w_gate, w_up, w_down):
    vmem = pl.BlockSpec(memory_space=pltpu.VMEM)
    hbm = pl.BlockSpec(memory_space=pl.ANY)
    up_spec = pl.BlockSpec((1, D, FF), lambda i, info: (i, 0, 0))
    down_spec = pl.BlockSpec((1, FF, D), lambda i, info: (i, 0, 0))
    own_d = pl.BlockSpec((1, OWN, D), lambda i, info: (i, 0, 0))
    own_f = pl.BlockSpec((1, OWN, FF), lambda i, info: (i, 0, 0))
    return pl.pallas_call(
        main_kernel,
        out_shape=(
            jax.ShapeDtypeStruct((E_LOC, D, FF), F32),
            jax.ShapeDtypeStruct((E_LOC, D, FF), F32),
            jax.ShapeDtypeStruct((E_LOC, FF, D), F32),
            jax.ShapeDtypeStruct((2, TOK, D), F32),
            jax.ShapeDtypeStruct((2, E_LOC, TOK), F32),
        ),
        grid_spec=pltpu.PrefetchScalarGridSpec(
            num_scalar_prefetch=1,
            grid=(E_LOC,),
            in_specs=[hbm, hbm, vmem, vmem, hbm, vmem, own_d, own_d, own_f, own_f, own_f, up_spec, up_spec, down_spec],
            out_specs=(up_spec, up_spec, down_spec, vmem, vmem),
            scratch_shapes=[
                pltpu.VMEM((SHARDS, TOK, D), BF16),
                pltpu.VMEM((SHARDS, TOK, D), BF16),
                pltpu.VMEM((SHARDS, EXPERTS, TOK), F32),
                pltpu.VMEM((SHARDS, EXPERTS, TOK), F32),
                pltpu.SMEM((SHARDS,), jnp.int32),
                pltpu.SMEM((SHARDS,), jnp.int32),
                pltpu.VMEM((2, GROUP, ROWS, D), BF16),
                pltpu.VMEM((2, GROUP, ROWS, D), BF16),
                pltpu.VMEM((ROWS, D), BF16),
                pltpu.VMEM((ROWS, D), BF16),
                pltpu.VMEM((2 * HOT, D), BF16),
                pltpu.VMEM((ROWS, FF), BF16),
                pltpu.VMEM((ROWS, FF), BF16),
                pltpu.VMEM((ROWS, FF), BF16),
                pltpu.SemaphoreType.DMA((3, SHARDS)),
            ],
        ),
        compiler_params=pltpu.CompilerParams(
            dimension_semantics=("arbitrary",), vmem_limit_bytes=VMEM_ALL),
        cost_estimate=pl.CostEstimate(flops=70_000_000_000, bytes_accessed=180_000_000, transcendentals=8_000_000),
        name="experts",
    )(info, x_all, g_all, idx_all, w_router_t, s_part, q_part, *own, w_gate, w_up, w_down)


def peer(step):
    chip = lax.axis_index("dp")
    core = lax.axis_index("ep")
    x_bit, y_bit = lax.rem(chip, 2), lax.div(chip, 2)
    if step & 2:
        x_bit = 1 - x_bit
    if step & 4:
        y_bit = 1 - y_bit
    if step & 1:
        core = 1 - core
    return {"dp": 2 * y_bit + x_bit, "ep": core}


def greet_all():
    barrier = pltpu.get_barrier_semaphore()
    for step in range(1, SHARDS):
        pl.semaphore_signal(barrier, inc=1, device_id=peer(step), device_id_type=MESH)
    pl.semaphore_wait(barrier, SHARDS - 1)


def share_kernel(x_ref, g_ref, idx_ref, wr_ref, w1_ref, w3_ref, w2_ref,
                 x_all, g_all, idx_all, s_ref, q_ref, gate_ref, own_x, own_do, own_a, own_dz1, own_dz3,
                 x_par, g_par, idx_par, code_s, gate_s, xg_s, do_s, gg_s, r_s, send, recv, local):
    i = pl.program_id(0)
    e = lax.axis_index("ep") * E_LOC + i
    j = lax.rem(i, GROUP)

    def copy(ref, into, sem, step):
        return pltpu.make_async_remote_copy(
            src_ref=ref, dst_ref=into, send_sem=send.at[sem], recv_sem=recv.at[sem],
            device_id=peer(step), device_id_type=MESH)

    own = [pltpu.make_async_copy(ref, into.at[0], local.at[n])
           for n, (ref, into) in enumerate(((x_ref, x_all), (g_ref, g_all), (idx_ref, idx_all)))]
    par = [pltpu.make_async_copy(ref, into.at[1], local.at[3 + n])
           for n, (ref, into) in enumerate(((x_par, x_all), (g_par, g_all), (idx_par, idx_all)))]
    x1, g1, id1 = copy(x_ref, x_par, 0, 1), copy(g_ref, g_par, 7, 1), copy(idx_ref, idx_par, 14, 1)
    ids = [copy(idx_ref, idx_all.at[k], 14 + k - 1, k) for k in range(2, SHARDS)]
    x2, g2 = copy(x_ref, x_all.at[2], 1, 2), copy(g_ref, g_all.at[2], 8, 2)
    g4, x4 = copy(g_ref, g_all.at[4], 10, 4), copy(x_ref, x_all.at[4], 3, 4)
    x6, g6 = copy(x_all.at[2], x_all.at[6], 5, 4), copy(g_all.at[4], g_all.at[6], 12, 2)
    x3, g3 = copy(x_all.at[2], x_all.at[3], 2, 1), copy(g_all.at[2], g_all.at[3], 9, 1)
    x5, g5 = copy(x_all.at[4], x_all.at[5], 4, 1), copy(g_all.at[4], g_all.at[5], 11, 1)
    x7, g7 = copy(x_all.at[6], x_all.at[7], 6, 1), copy(g_all.at[6], g_all.at[7], 13, 1)

    @pl.when(i == 0)
    def _():
        greet_all()
        for c in (id1, x2, g4, x1, g1, g2, x4, *ids):
            c.start()
        for c in own:
            c.start()
        s_ref[...] = jnp.zeros_like(s_ref)
        code, gates, _ = route_tables(x_ref[...], idx_ref[...], wr_ref[...])
        code_s[0] = code
        gate_s[0] = gates
        gate_ref[...] = gates
        id1.wait_recv()
        x1.wait_recv()
        g1.wait_recv()
        for c in par:
            c.start()
        code, gates, _ = route_tables(x_par[...], idx_par[...], wr_ref[...])
        code_s[1] = code
        gate_s[1] = gates

    @pl.when(i == FORWARD[0])
    def _():
        x2.wait_recv()
        g4.wait_recv()
        for c in (x6, g6, x3, g5):
            c.start()

    @pl.when(i == FORWARD[1])
    def _():
        g2.wait_recv()
        x4.wait_recv()
        g3.start()
        x5.start()

    @pl.when(i == FORWARD[2])
    def _():
        x6.wait_recv()
        x7.start()
        g6.wait_recv()
        g7.start()

    @pl.when(j == 0)
    def _():
        for b, (xb, gb) in enumerate(((x_ref, g_ref), (x_par, g_par))):
            masks = [slot_mask(code_s[b, pl.ds(e + jj, 1), :], SLOT, 0.0) for jj in range(GROUP)]
            sel = jnp.concatenate([as_bf16(m) for m in masks], axis=0)
            xg = dot_nn(sel, xb[...]).astype(BF16)
            gg = dot_nn(sel, gb[...])
            rows = slice(b * SLOT, (b + 1) * SLOT)
            for jj in range(GROUP):
                part = slice(jj * SLOT, (jj + 1) * SLOT)
                xg_s[jj, rows, :] = xg[part]
                gg_s[jj, rows, :] = gg[part].astype(BF16)
                p_col = jnp.sum(jnp.where(masks[jj], gate_s[b, pl.ds(e + jj, 1), :], 0.0), axis=1, keepdims=True)
                do_s[jj, rows, :] = (p_col * gg[part]).astype(BF16)

    z1 = dot_nn(xg_s[j], w1_ref[0])
    z3 = dot_nn(xg_s[j], w3_ref[0])
    da = dot_nt(do_s[j], w2_ref[0])
    act, dz1, dz3 = swiglu_grads(z1, z3, da)
    own_x[0] = xg_s[j]
    own_do[0] = do_s[j]
    own_a[0] = act
    own_dz1[0] = dz1
    own_dz3[0] = dz3
    o = dot_nn(act, w2_ref[0])
    q = jnp.sum(o * gg_s[j].astype(F32), axis=1, keepdims=True)
    for b in range(2):
        mask = slot_mask(code_s[b, pl.ds(e, 1), :], SLOT, 0.0)
        q_ref[b, pl.ds(i, 1), :] = jnp.sum(jnp.where(mask, q[b * SLOT:(b + 1) * SLOT], 0.0), axis=0, keepdims=True)
    odd = lax.rem(i, 2)
    dx_t = dot_nt(w1_ref[0], dz1) + dot_nt(w3_ref[0], dz3)
    r_s[:, pl.ds(pl.multiple_of(odd * OWN, OWN), OWN)] = dx_t.astype(BF16)

    @pl.when(odd == 1)
    def _():
        zero = jnp.zeros((SLOT, TOK), BF16)
        rows = []
        for ex in (e - 1, e):
            first, second = (as_bf16(slot_mask(code_s[b, pl.ds(ex, 1), :], SLOT, 0.0)) for b in range(2))
            rows += [jnp.concatenate([first, zero], axis=1), jnp.concatenate([zero, second], axis=1)]
        part = lax.dot_general(jnp.concatenate(rows, axis=0), r_s[...], (((0,), (1,)), ((), ())), preferred_element_type=F32)
        for b in range(2):
            s_ref[b] += part[b * TOK:(b + 1) * TOK]

    @pl.when(i == E_LOC - 1)
    def _():
        for c in (x3, g3, x5, g5, x7, g7, *ids):
            c.wait_recv()
        for c in (x1, g1, id1, x2, g2, g4, x4, x6, g6, x3, g3, x5, g5, x7, g7, *ids):
            c.wait_send()
        for c in own + par:
            c.wait()


def share_tokens(x_loc, dy_loc, idx_t, w_router_t, w_gate, w_up, w_down):
    vmem = pl.BlockSpec(memory_space=pltpu.VMEM)
    hbm = pl.BlockSpec(memory_space=pl.ANY)
    up_spec = pl.BlockSpec((1, D, FF), lambda i: (i, 0, 0))
    down_spec = pl.BlockSpec((1, FF, D), lambda i: (i, 0, 0))
    own_d = pl.BlockSpec((1, OWN, D), lambda i: (i, 0, 0))
    own_f = pl.BlockSpec((1, OWN, FF), lambda i: (i, 0, 0))
    return pl.pallas_call(
        share_kernel,
        out_shape=(
            jax.ShapeDtypeStruct((SHARDS, TOK, D), BF16),
            jax.ShapeDtypeStruct((SHARDS, TOK, D), BF16),
            jax.ShapeDtypeStruct((SHARDS, TOP, TOK), jnp.int32),
            jax.ShapeDtypeStruct((2, TOK, D), F32),
            jax.ShapeDtypeStruct((2, E_LOC, TOK), F32),
            jax.ShapeDtypeStruct((EXPERTS, TOK), F32),
            jax.ShapeDtypeStruct((E_LOC, OWN, D), BF16),
            jax.ShapeDtypeStruct((E_LOC, OWN, D), BF16),
            jax.ShapeDtypeStruct((E_LOC, OWN, FF), BF16),
            jax.ShapeDtypeStruct((E_LOC, OWN, FF), BF16),
            jax.ShapeDtypeStruct((E_LOC, OWN, FF), BF16),
        ),
        grid=(E_LOC,),
        in_specs=[vmem] * 4 + [up_spec, up_spec, down_spec],
        out_specs=(hbm, hbm, hbm, vmem, vmem, vmem, own_d, own_d, own_f, own_f, own_f),
        scratch_shapes=[
            pltpu.VMEM((TOK, D), BF16),
            pltpu.VMEM((TOK, D), BF16),
            pltpu.VMEM((TOP, TOK), jnp.int32),
            pltpu.VMEM((2, EXPERTS, TOK), F32),
            pltpu.VMEM((2, EXPERTS, TOK), F32),
            pltpu.VMEM((GROUP, OWN, D), BF16),
            pltpu.VMEM((GROUP, OWN, D), BF16),
            pltpu.VMEM((GROUP, OWN, D), BF16),
            pltpu.VMEM((D, 2 * OWN), BF16),
            pltpu.SemaphoreType.DMA((21,)),
            pltpu.SemaphoreType.DMA((21,)),
            pltpu.SemaphoreType.DMA((6,)),
        ],
        compiler_params=pltpu.CompilerParams(
            dimension_semantics=("arbitrary",), collective_id=0, has_side_effects=True, vmem_limit_bytes=VMEM_ALL),
        cost_estimate=pl.CostEstimate(flops=20_000_000_000, bytes_accessed=70_000_000, transcendentals=2_000_000),
        name="share",
    )(x_loc, dy_loc, idx_t, w_router_t, w_gate, w_up, w_down)


def tail_kernel(s_hbm, q_hbm, gate_hbm, x_hbm, wr_ref, gx_ref, gr_ref,
                s_own, s_got, q_own, q_got, gate_s, x_all, dl_all, send, recv, local):
    core = lax.axis_index("ep")

    def copy(ref, into, sem, step):
        return pltpu.make_async_remote_copy(
            src_ref=ref, dst_ref=into, send_sem=send.at[sem], recv_sem=recv.at[sem],
            device_id=peer(step), device_id_type=MESH)

    loads = [pltpu.make_async_copy(ref, into, local.at[n]) for n, (ref, into) in enumerate(
        ((q_hbm.at[0], q_own), (gate_hbm, gate_s), (s_hbm.at[0], s_own), (x_hbm, x_all)))]
    for c in loads:
        c.start()
    greet_all()
    q_copy = copy(q_hbm.at[1], q_got, 0, 1)
    s_copy = copy(s_hbm.at[1], s_got, 1, 1)
    q_copy.start()
    s_copy.start()
    loads[0].wait()
    loads[1].wait()
    q_copy.wait_recv()
    low = jnp.concatenate([q_own[...], q_got[...]], axis=0)
    high = jnp.concatenate([q_got[...], q_own[...]], axis=0)
    q = jnp.where(core == 0, low, high)
    p = gate_s[...]
    d_log = (p * (q - jnp.sum(p * q, axis=0, keepdims=True))).astype(BF16)
    dl_all[0] = d_log
    copies = [copy(dl_all.at[0], dl_all.at[k], 1 + k, k) for k in range(1, SHARDS)]
    for c in copies:
        c.start()
    du = dot_tn(d_log, wr_ref[...])
    loads[2].wait()
    s_copy.wait_recv()
    gx_ref[...] = (s_own[...] + s_got[...] + du).astype(BF16)
    loads[3].wait()
    total = dot_nn(d_log, x_all[0])
    for k in range(1, SHARDS):
        copies[k - 1].wait_recv()
        total += dot_nn(dl_all[k], x_all[k])
    gr_ref[...] = total
    q_copy.wait_send()
    s_copy.wait_send()
    for c in copies:
        c.wait_send()


def tail(dx_part, q_part, gates, x_all, w_router_t):
    vmem = pl.BlockSpec(memory_space=pltpu.VMEM)
    hbm = pl.BlockSpec(memory_space=pl.ANY)
    return pl.pallas_call(
        tail_kernel,
        out_shape=(jax.ShapeDtypeStruct((TOK, D), BF16), jax.ShapeDtypeStruct((EXPERTS, D), F32)),
        in_specs=[hbm] * 4 + [vmem],
        out_specs=(vmem, vmem),
        scratch_shapes=[
            pltpu.VMEM((TOK, D), F32),
            pltpu.VMEM((TOK, D), F32),
            pltpu.VMEM((E_LOC, TOK), F32),
            pltpu.VMEM((E_LOC, TOK), F32),
            pltpu.VMEM((EXPERTS, TOK), F32),
            pltpu.VMEM((SHARDS, TOK, D), BF16),
            pltpu.VMEM((SHARDS, EXPERTS, TOK), BF16),
            pltpu.SemaphoreType.DMA((9,)),
            pltpu.SemaphoreType.DMA((9,)),
            pltpu.SemaphoreType.DMA((4,)),
        ],
        compiler_params=pltpu.CompilerParams(collective_id=1, has_side_effects=True, vmem_limit_bytes=62_000_000),
        name="tail",
    )(dx_part, q_part, gates, x_all, w_router_t)


def solution(mesh):
    tok_spec = P(("dp", "ep"), None)
    exp_spec = P("ep", None, None)

    def device_step(x_loc, route_idx, w_router, w_gate, w_up, w_down, dy_loc):
        info = lax.axis_index("ep").astype(jnp.int32).reshape(1)
        w_router_t = w_router.T
        x_all, g_all, idx_all, dx_own, q_own, gates, *own = share_tokens(
            x_loc, dy_loc, route_idx.T, w_router_t, w_gate, w_up, w_down)
        g1, g3, g2, dx_part, q_part = expert_pass(
            info, x_all, g_all, idx_all, w_router_t, dx_own, q_own, own, w_gate, w_up, w_down)
        grad_x, grad_router_t = tail(dx_part, q_part, gates, x_all, w_router_t)
        return grad_x, g1, g3, g2, grad_router_t.T

    return jax.shard_map(device_step, mesh=mesh, in_specs=(tok_spec, tok_spec, P(), exp_spec, exp_spec, exp_spec, tok_spec), out_specs=(tok_spec, exp_spec, exp_spec, exp_spec, P()), check_vma=False)
```

time: 173 us -> 150 us (0.87)
  Pallas kernels: 163 us -> 145 us
  local copies, waits for them, and re-layouts: 8.68 us -> 3.44 us
    pallas_call x1, Pallas kernels: 111 us -> 87.8 us  [expert_pass(): pl.pallas_call(main_kernel, out_shape=(jax.ShapeDtypeStruct((E_LOC, D, FF...]
    unnamed x13 -> x2, local copies, waits for them, and re-layouts: 8.68 us -> 3.44 us
    pallas_call x1, Pallas kernels: 44.1 us -> 49.1 us  [share_tokens(): pl.pallas_call(share_kernel, out_shape=(jax.ShapeDtypeStruct((SHARDS, TOK...]
where the time goes in v2:
time: 150 us; the launch traced here: 149 us
  Pallas kernels  145 us (97%)
  local copies, waits for them, and re-layouts  3.44 us (2%)
    pallas_call x1, Pallas kernels, expert_pass(): pl.pallas_call(main_kernel, out_shape=(jax.ShapeDtypeStruct((E_LOC, D, FF...  87.8 us
    pallas_call x1, Pallas kernels, share_tokens(): pl.pallas_call(share_kernel, out_shape=(jax.ShapeDtypeStruct((SHARDS, TOK...  49.1 us
    pallas_call x1, Pallas kernels, tail(): pl.pallas_call(tail_kernel, out_shape=(jax.ShapeDtypeStruct((TOK, D), BF1...  8.41 us
    unnamed x2, local copies, waits for them, and re-layouts  3.44 us

profile of v2, /device:TPU:0, one launch (start us, length us, event | category | flops | bytes accessed | tf_op | source)
XLA Modules:
  0.0 149.4 jit_solution(11016378763587001765)
XLA Ops:
  0.6 49.1 %share.1 = (bf16[8,256,1024]{2,1,0:T(8,128)(2,1)}, bf16[8,256,1024]{2,1,0:T(8,128)(2,1)}, s32[8,8,256]{2,1,0:T(8,128)}, f32[2,256,1024]{2,1,0:T(8,128)}, f32[2,1...) custom-call(bf16[256,1024]{1,0:T(8,128)(2,1)} %x_ref.1, ...), custom_call_target="tpu_custom_call" | custom-call | flops 20000000000 | bytes 70000000 | tf_op jit(solution)/shard_map/share/pallas_call | solution.py:414
  49.7 87.8 %experts.1 = (f32[16,1024,512]{2,1,0:T(8,128)}, f32[16,1024,512]{2,1,0:T(8,128)}, f32[16,512,1024]{2,1,0:T(8,128)}, f32[2,256,1024]{2,1,0:T(8,128)}, f32[2,16,256]{2,1,0:T(8,128)}) custom-call(s32[1]{0:T(128)} %bitcast.info, bf16[8,256,1024]{2,1,0:T(8,128)(2,1)} %get-tuple-element.23.x_hbm, bf16[8,256,1024]{2,1,0:T(8,128)(2,1)} %get-tuple-element.24.g_hbm, ...), custom_call_target="tpu_custom_call" | custom-call | flops 70000001024 | bytes 180000000 | tf_op jit(solution)/shard_map/experts/pallas_call | solution.py:227
  137.5 8.4 %tail.1 = (bf16[256,1024]{1,0:T(8,128)(2,1)}, f32[32,1024]{1,0:T(8,128)}) custom-call(f32[2,256,1024]{2,1,0:T(8,128)} %get-tuple-element.33.s_hbm, f32[2,16,256]{2,1,0:T(8,128)} %get-tuple-element.34.q_hbm, f32[32,256]{1,0:T(8,128)} %get-tuple-element.35.gate_hbm, bf16[8,256,1024]{2,1,0:T(8,128)(2,1)} %get-tuple-element.23.x_hbm, bf16[32,1024]{1,0:T(8,128)(2,1)} %bitcast.7), custom_call_target="tpu_custom_call" | custom-call | tf_op jit(solution)/shard_map/tail/pallas_call | solution.py:502
  145.9 1.9 %copy.14 = bf16[256,1024]{1,0:T(8,128)(2,1)} copy(bf16[256,1024]{1,0:T(8,128)(2,1)} %get-tuple-element.46) | data formatting | bytes 1048576
  147.8 1.6 %copy.15 = f32[1024,32]{0,1:T(8,128)} copy(f32[1024,32]{0,1:T(8,128)} %bitcast.4) | data formatting | bytes 262144

commit v3 on v2

--- a/solution.py
+++ b/solution.py
@@ -80,8 +80,8 @@
 
 
 def main_kernel(info, x_hbm, g_hbm, idx_ref, wr_ref, s_hbm, q_in, own_x, own_do, own_a, own_dz1, own_dz3,
-                w1_ref, w3_ref, w2_ref, o1_ref, o3_ref, o2_ref, s_ref, q_ref,
-                x_s, g_s, code_s, gate_s, hot_s, list_s, xg_s, do_s, xh_s, dh_s, gg_s, a_s, dz1_s, dz3_s, sem):
+                w1_ref, w3_ref, w2_ref, o1_ref, o3_ref, o2_ref, s_ref, q_ref, gate_s,
+                x_s, g_s, code_s, hot_s, list_s, xg_s, do_s, xh_s, dh_s, gg_s, a_s, dz1_s, dz3_s, sem):
     i = pl.program_id(0)
     e = info[0] * E_LOC + i
     j = lax.rem(i, GROUP)
@@ -180,23 +180,22 @@
         n_hot = n_hot + hit.astype(jnp.int32)
 
     def hot_chunk(c, _):
-        def hot_gather(k, _):
+        def hot_gather(k):
             pos = c * 4 + k
             b = list_s[pos]
             live = pos < n_hot
             mask = select(b, e, HOT, jnp.where(live, float(SLOT), 4096.0))
             sel = as_bf16(mask)
-            rows = pl.ds(pl.multiple_of(k * HOT, HOT), HOT)
+            rows = slice(k * HOT, (k + 1) * HOT)
             xh_s[rows, :] = dot_nn(sel, x_s[b]).astype(BF16)
             gg = dot_nn(sel, g_s[b])
             p_col = jnp.sum(jnp.where(mask, gate_s[b, pl.ds(e, 1), :], 0.0), axis=1, keepdims=True)
             dh_s[rows, :] = (p_col * gg).astype(BF16)
 
-            @pl.when(k < 2)
-            def _():
+            if k < 2:
                 gg_s[rows, :] = gg.astype(BF16)
-            return 0
-        lax.fori_loop(0, 4, hot_gather, 0)
+        for k in range(4):
+            hot_gather(k)
         compute(xh_s, dh_s, False)
 
         @pl.when((c == 0) & (list_s[0] < 2))
@@ -232,16 +231,16 @@
             jax.ShapeDtypeStruct((E_LOC, FF, D), F32),
             jax.ShapeDtypeStruct((2, TOK, D), F32),
             jax.ShapeDtypeStruct((2, E_LOC, TOK), F32),
+            jax.ShapeDtypeStruct((SHARDS, EXPERTS, TOK), F32),
         ),
         grid_spec=pltpu.PrefetchScalarGridSpec(
             num_scalar_prefetch=1,
             grid=(E_LOC,),
             in_specs=[hbm, hbm, vmem, vmem, hbm, vmem, own_d, own_d, own_f, own_f, own_f, up_spec, up_spec, down_spec],
-            out_specs=(up_spec, up_spec, down_spec, vmem, vmem),
+            out_specs=(up_spec, up_spec, down_spec, vmem, vmem, vmem),
             scratch_shapes=[
                 pltpu.VMEM((SHARDS, TOK, D), BF16),
                 pltpu.VMEM((SHARDS, TOK, D), BF16),
-                pltpu.VMEM((SHARDS, EXPERTS, TOK), F32),
                 pltpu.VMEM((SHARDS, EXPERTS, TOK), F32),
                 pltpu.SMEM((SHARDS,), jnp.int32),
                 pltpu.SMEM((SHARDS,), jnp.int32),
@@ -283,9 +282,10 @@
     pl.semaphore_wait(barrier, SHARDS - 1)
 
 
-def share_kernel(x_ref, g_ref, idx_ref, wr_ref, w1_ref, w3_ref, w2_ref,
-                 x_all, g_all, idx_all, s_ref, q_ref, gate_ref, own_x, own_do, own_a, own_dz1, own_dz3,
-                 x_par, g_par, idx_par, code_s, gate_s, xg_s, do_s, gg_s, r_s, send, recv, local):
+def share_kernel(x_hbm, g_hbm, idx_ref, wr_ref, w1_hbm, w3_hbm, w2_hbm,
+                 x_all, g_all, idx_all, s_ref, q_ref, own_x, own_do, own_a, own_dz1, own_dz3,
+                 x_ref, g_ref, x_par, g_par, idx_par, code_s, gate_s, xg_s, do_s, gg_s, r_s, w1_s, w3_s, w2_s,
+                 send, recv, local, w_sem):
     i = pl.program_id(0)
     e = lax.axis_index("ep") * E_LOC + i
     j = lax.rem(i, GROUP)
@@ -299,10 +299,17 @@
            for n, (ref, into) in enumerate(((x_ref, x_all), (g_ref, g_all), (idx_ref, idx_all)))]
     par = [pltpu.make_async_copy(ref, into.at[1], local.at[3 + n])
            for n, (ref, into) in enumerate(((x_par, x_all), (g_par, g_all), (idx_par, idx_all)))]
-    x1, g1, id1 = copy(x_ref, x_par, 0, 1), copy(g_ref, g_par, 7, 1), copy(idx_ref, idx_par, 14, 1)
+    takes = [pltpu.make_async_copy(x_hbm, x_ref, local.at[6]), pltpu.make_async_copy(g_hbm, g_ref, local.at[7])]
+
+    def weights(step, to):
+        return [pltpu.make_async_copy(ref.at[step], into.at[to], w_sem.at[n, to])
+                for n, (ref, into) in enumerate(((w1_hbm, w1_s), (w3_hbm, w3_s), (w2_hbm, w2_s)))]
+
+    now = lax.rem(i, 2)
+    x1, g1, id1 = copy(x_hbm, x_par, 0, 1), copy(g_hbm, g_par, 7, 1), copy(idx_ref, idx_par, 14, 1)
     ids = [copy(idx_ref, idx_all.at[k], 14 + k - 1, k) for k in range(2, SHARDS)]
-    x2, g2 = copy(x_ref, x_all.at[2], 1, 2), copy(g_ref, g_all.at[2], 8, 2)
-    g4, x4 = copy(g_ref, g_all.at[4], 10, 4), copy(x_ref, x_all.at[4], 3, 4)
+    x2, g2 = copy(x_hbm, x_all.at[2], 1, 2), copy(g_hbm, g_all.at[2], 8, 2)
+    g4, x4 = copy(g_hbm, g_all.at[4], 10, 4), copy(x_hbm, x_all.at[4], 3, 4)
     x6, g6 = copy(x_all.at[2], x_all.at[6], 5, 4), copy(g_all.at[4], g_all.at[6], 12, 2)
     x3, g3 = copy(x_all.at[2], x_all.at[3], 2, 1), copy(g_all.at[2], g_all.at[3], 9, 1)
     x5, g5 = copy(x_all.at[4], x_all.at[5], 4, 1), copy(g_all.at[4], g_all.at[5], 11, 1)
@@ -310,16 +317,21 @@
 
     @pl.when(i == 0)
     def _():
+        for c in takes:
+            c.start()
         greet_all()
-        for c in (id1, x2, g4, x1, g1, g2, x4, *ids):
-            c.start()
+        for c in (x2, g4, id1, x1, g1, g2, x4, *ids):
+            c.start()
+        for c in weights(0, 0):
+            c.start()
+        for c in takes:
+            c.wait()
         for c in own:
             c.start()
         s_ref[...] = jnp.zeros_like(s_ref)
         code, gates, _ = route_tables(x_ref[...], idx_ref[...], wr_ref[...])
         code_s[0] = code
         gate_s[0] = gates
-        gate_ref[...] = gates
         id1.wait_recv()
         x1.wait_recv()
         g1.wait_recv()
@@ -365,22 +377,30 @@
                 p_col = jnp.sum(jnp.where(masks[jj], gate_s[b, pl.ds(e + jj, 1), :], 0.0), axis=1, keepdims=True)
                 do_s[jj, rows, :] = (p_col * gg[part]).astype(BF16)
 
-    z1 = dot_nn(xg_s[j], w1_ref[0])
-    z3 = dot_nn(xg_s[j], w3_ref[0])
-    da = dot_nt(do_s[j], w2_ref[0])
+    for c in weights(i, now):
+        c.wait()
+
+    @pl.when(i < E_LOC - 1)
+    def _():
+        for c in weights(i + 1, 1 - now):
+            c.start()
+
+    z1 = dot_nn(xg_s[j], w1_s[now])
+    z3 = dot_nn(xg_s[j], w3_s[now])
+    da = dot_nt(do_s[j], w2_s[now])
     act, dz1, dz3 = swiglu_grads(z1, z3, da)
     own_x[0] = xg_s[j]
     own_do[0] = do_s[j]
     own_a[0] = act
     own_dz1[0] = dz1
     own_dz3[0] = dz3
-    o = dot_nn(act, w2_ref[0])
+    o = dot_nn(act, w2_s[now])
     q = jnp.sum(o * gg_s[j].astype(F32), axis=1, keepdims=True)
     for b in range(2):
         mask = slot_mask(code_s[b, pl.ds(e, 1), :], SLOT, 0.0)
         q_ref[b, pl.ds(i, 1), :] = jnp.sum(jnp.where(mask, q[b * SLOT:(b + 1) * SLOT], 0.0), axis=0, keepdims=True)
     odd = lax.rem(i, 2)
-    dx_t = dot_nt(w1_ref[0], dz1) + dot_nt(w3_ref[0], dz3)
+    dx_t = dot_nt(w1_s[now], dz1) + dot_nt(w3_s[now], dz3)
     r_s[:, pl.ds(pl.multiple_of(odd * OWN, OWN), OWN)] = dx_t.astype(BF16)
 
     @pl.when(odd == 1)
@@ -407,8 +427,6 @@
 def share_tokens(x_loc, dy_loc, idx_t, w_router_t, w_gate, w_up, w_down):
     vmem = pl.BlockSpec(memory_space=pltpu.VMEM)
     hbm = pl.BlockSpec(memory_space=pl.ANY)
-    up_spec = pl.BlockSpec((1, D, FF), lambda i: (i, 0, 0))
-    down_spec = pl.BlockSpec((1, FF, D), lambda i: (i, 0, 0))
     own_d = pl.BlockSpec((1, OWN, D), lambda i: (i, 0, 0))
     own_f = pl.BlockSpec((1, OWN, FF), lambda i: (i, 0, 0))
     return pl.pallas_call(
@@ -419,7 +437,6 @@
             jax.ShapeDtypeStruct((SHARDS, TOP, TOK), jnp.int32),
             jax.ShapeDtypeStruct((2, TOK, D), F32),
             jax.ShapeDtypeStruct((2, E_LOC, TOK), F32),
-            jax.ShapeDtypeStruct((EXPERTS, TOK), F32),
             jax.ShapeDtypeStruct((E_LOC, OWN, D), BF16),
             jax.ShapeDtypeStruct((E_LOC, OWN, D), BF16),
             jax.ShapeDtypeStruct((E_LOC, OWN, FF), BF16),
@@ -427,9 +444,11 @@
             jax.ShapeDtypeStruct((E_LOC, OWN, FF), BF16),
         ),
         grid=(E_LOC,),
-        in_specs=[vmem] * 4 + [up_spec, up_spec, down_spec],
-        out_specs=(hbm, hbm, hbm, vmem, vmem, vmem, own_d, own_d, own_f, own_f, own_f),
+        in_specs=[hbm, hbm, vmem, vmem, hbm, hbm, hbm],
+        out_specs=(hbm, hbm, hbm, vmem, vmem, own_d, own_d, own_f, own_f, own_f),
         scratch_shapes=[
+            pltpu.VMEM((TOK, D), BF16),
+            pltpu.VMEM((TOK, D), BF16),
             pltpu.VMEM((TOK, D), BF16),
             pltpu.VMEM((TOK, D), BF16),
             pltpu.VMEM((TOP, TOK), jnp.int32),
@@ -439,9 +458,13 @@
             pltpu.VMEM((GROUP, OWN, D), BF16),
             pltpu.VMEM((GROUP, OWN, D), BF16),
             pltpu.VMEM((D, 2 * OWN), BF16),
+            pltpu.VMEM((2, D, FF), BF16),
+            pltpu.VMEM((2, D, FF), BF16),
+            pltpu.VMEM((2, FF, D), BF16),
             pltpu.SemaphoreType.DMA((21,)),
             pltpu.SemaphoreType.DMA((21,)),
-            pltpu.SemaphoreType.DMA((6,)),
+            pltpu.SemaphoreType.DMA((8,)),
+            pltpu.SemaphoreType.DMA((3, 2)),
         ],
         compiler_params=pltpu.CompilerParams(
             dimension_semantics=("arbitrary",), collective_id=0, has_side_effects=True, vmem_limit_bytes=VMEM_ALL),
@@ -451,7 +474,7 @@
 
 
 def tail_kernel(s_hbm, q_hbm, gate_hbm, x_hbm, wr_ref, gx_ref, gr_ref,
-                s_own, s_got, q_own, q_got, gate_s, x_all, dl_all, send, recv, local):
+                s_own, s_got, q_all, gate_s, x_all, send, recv, local):
     core = lax.axis_index("ep")
 
     def copy(ref, into, sem, step):
@@ -460,37 +483,38 @@
             device_id=peer(step), device_id_type=MESH)
 
     loads = [pltpu.make_async_copy(ref, into, local.at[n]) for n, (ref, into) in enumerate(
-        ((q_hbm.at[0], q_own), (gate_hbm, gate_s), (s_hbm.at[0], s_own), (x_hbm, x_all)))]
-    for c in loads:
+        ((q_hbm, q_all.at[0]), (gate_hbm, gate_s), (s_hbm.at[0], s_own), (x_hbm, x_all)))]
+    for c in loads[:2]:
         c.start()
     greet_all()
-    q_copy = copy(q_hbm.at[1], q_got, 0, 1)
-    s_copy = copy(s_hbm.at[1], s_got, 1, 1)
-    q_copy.start()
+    loads[0].wait()
+    copies = [copy(q_all.at[0], q_all.at[k], k, k) for k in range(1, SHARDS)]
+    for k in (6, 7, 2, 3, 4, 5, 1):
+        copies[k - 1].start()
+    s_copy = copy(s_hbm.at[1], s_got, 0, 1)
     s_copy.start()
-    loads[0].wait()
+    for c in loads[2:]:
+        c.start()
+    def d_logits(k, n):
+        near, far = q_all[k, n], q_all[k + 1, 1 - n]
+        low = jnp.concatenate([near, far], axis=0)
+        high = jnp.concatenate([far, near], axis=0)
+        q = jnp.where(core == 0, low, high)
+        p = gate_s[k + n]
+        return (p * (q - jnp.sum(p * q, axis=0, keepdims=True))).astype(BF16)
+
     loads[1].wait()
-    q_copy.wait_recv()
-    low = jnp.concatenate([q_own[...], q_got[...]], axis=0)
-    high = jnp.concatenate([q_got[...], q_own[...]], axis=0)
-    q = jnp.where(core == 0, low, high)
-    p = gate_s[...]
-    d_log = (p * (q - jnp.sum(p * q, axis=0, keepdims=True))).astype(BF16)
-    dl_all[0] = d_log
-    copies = [copy(dl_all.at[0], dl_all.at[k], 1 + k, k) for k in range(1, SHARDS)]
-    for c in copies:
-        c.start()
+    copies[0].wait_recv()
+    d_log = d_logits(0, 0)
     du = dot_tn(d_log, wr_ref[...])
     loads[2].wait()
     s_copy.wait_recv()
     gx_ref[...] = (s_own[...] + s_got[...] + du).astype(BF16)
     loads[3].wait()
-    total = dot_nn(d_log, x_all[0])
-    for k in range(1, SHARDS):
+    for k in range(2, SHARDS):
         copies[k - 1].wait_recv()
-        total += dot_nn(dl_all[k], x_all[k])
-    gr_ref[...] = total
-    q_copy.wait_send()
+    every = jnp.concatenate([d_log] + [d_logits(k - k % 2, k % 2) for k in range(1, SHARDS)], axis=1)
+    gr_ref[...] = dot_nn(every, x_all[...])
     s_copy.wait_send()
     for c in copies:
         c.wait_send()
@@ -507,18 +531,16 @@
         scratch_shapes=[
             pltpu.VMEM((TOK, D), F32),
             pltpu.VMEM((TOK, D), F32),
-            pltpu.VMEM((E_LOC, TOK), F32),
-            pltpu.VMEM((E_LOC, TOK), F32),
-            pltpu.VMEM((EXPERTS, TOK), F32),
-            pltpu.VMEM((SHARDS, TOK, D), BF16),
-            pltpu.VMEM((SHARDS, EXPERTS, TOK), BF16),
-            pltpu.SemaphoreType.DMA((9,)),
-            pltpu.SemaphoreType.DMA((9,)),
+            pltpu.VMEM((SHARDS, 2, E_LOC, TOK), F32),
+            pltpu.VMEM((SHARDS, EXPERTS, TOK), F32),
+            pltpu.VMEM((SHARDS * TOK, D), BF16),
+            pltpu.SemaphoreType.DMA((SHARDS,)),
+            pltpu.SemaphoreType.DMA((SHARDS,)),
             pltpu.SemaphoreType.DMA((4,)),
         ],
         compiler_params=pltpu.CompilerParams(collective_id=1, has_side_effects=True, vmem_limit_bytes=62_000_000),
         name="tail",
-    )(dx_part, q_part, gates, x_all, w_router_t)
+    )(dx_part, q_part, gates, x_all.reshape(SHARDS * TOK, D), w_router_t)
 
 
 def solution(mesh):
@@ -528,9 +550,9 @@
     def device_step(x_loc, route_idx, w_router, w_gate, w_up, w_down, dy_loc):
         info = lax.axis_index("ep").astype(jnp.int32).reshape(1)
         w_router_t = w_router.T
-        x_all, g_all, idx_all, dx_own, q_own, gates, *own = share_tokens(
+        x_all, g_all, idx_all, dx_own, q_own, *own = share_tokens(
             x_loc, dy_loc, route_idx.T, w_router_t, w_gate, w_up, w_down)
-        g1, g3, g2, dx_part, q_part = expert_pass(
+        g1, g3, g2, dx_part, q_part, gates = expert_pass(
             info, x_all, g_all, idx_all, w_router_t, dx_own, q_own, own, w_gate, w_up, w_down)
         grad_x, grad_router_t = tail(dx_part, q_part, gates, x_all, w_router_t)
         return grad_x, g1, g3, g2, grad_router_t.T

time: 150 us -> 148 us (0.987)
  no operation moved by 1% of the time
where the time goes in v3:
time: 148 us
  Pallas kernels  144 us (97%)
  local copies, waits for them, and re-layouts  3.44 us (2%)
    pallas_call x1, Pallas kernels, expert_pass(): pl.pallas_call(main_kernel, out_shape=(jax.ShapeDtypeStruct((E_LOC, D, FF...  87.3 us
    pallas_call x1, Pallas kernels, share_tokens(): pl.pallas_call(share_kernel, out_shape=(jax.ShapeDtypeStruct((SHARDS, TOK...  47.7 us
    pallas_call x1, Pallas kernels, tail(): pl.pallas_call(tail_kernel, out_shape=(jax.ShapeDtypeStruct((TOK, D), BF1...  9.15 us
    unnamed x2, local copies, waits for them, and re-layouts  3.44 us

profile of v3, /device:TPU:0, one launch (start us, length us, event | category | flops | bytes accessed | tf_op | source)
XLA Modules:
  0.0 148.3 jit_solution(13310353735897293958)
XLA Ops:
  0.6 47.7 %share.1 = (bf16[8,256,1024]{2,1,0:T(8,128)(2,1)}, bf16[8,256,1024]{2,1,0:T(8,128)(2,1)}, s32[8,8,256]{2,1,0:T(8,128)}, f32[2,256,1024]{2,1,0:T(8,128)}, f32[2,1...) custom-call(bf16[256,1024]{1,0:T(8,128)(2,1)} %x_hbm.1, ...), custom_call_target="tpu_custom_call" | custom-call | flops 20000000000 | bytes 70000000 | tf_op jit(solution)/shard_map/share/pallas_call | solution.py:432
  48.4 87.3 %experts.1 = (f32[16,1024,512]{2,1,0:T(8,128)}, f32[16,1024,512]{2,1,0:T(8,128)}, f32[16,512,1024]{2,1,0:T(8,128)}, f32[2,256,1024]{2,1,0:T(8,128)}, f32[2,16,256]{2,1,0:T(8,128)}, /*index=5*/f32[8,32,256]{2,1,0:T(8,128)}) custom-call(s32[1]{0:T(128)} %bitcast.info, bf16[8,256,1024]{2,1,0:T(8,128)(2,1)} %get-tuple-element.23.x_hbm, ...), custom_call_target="tpu_custom_call" | custom-call | flops 70000001024 | bytes 180000000 | tf_op jit(solution)/shard_map/experts/pallas_call | solution.py:226
  135.7 9.2 %tail.1 = (bf16[256,1024]{1,0:T(8,128)(2,1)}, f32[32,1024]{1,0:T(8,128)}) custom-call(f32[2,256,1024]{2,1,0:T(8,128)} %get-tuple-element.33.s_hbm, f32[2,16,256]{2,1,0:T(8,128)} %get-tuple-element.34.q_hbm, f32[8,32,256]{2,1,0:T(8,128)} %get-tuple-element.35.gate_hbm, bf16[2048,1024]{1,0:T(8,128)(2,1)} %bitcast.5, bf16[32,1024]{1,0:T(8,128)(2,1)} %bitcast.9), custom_call_target="tpu_custom_call" | custom-call | tf_op jit(solution)/shard_map/tail/pallas_call | solution.py:526
  144.8 1.9 %copy.14 = bf16[256,1024]{1,0:T(8,128)(2,1)} copy(bf16[256,1024]{1,0:T(8,128)(2,1)} %get-tuple-element.46) | data formatting | bytes 1048576
  146.7 1.6 %copy.15 = f32[1024,32]{0,1:T(8,128)} copy(f32[1024,32]{0,1:T(8,128)} %bitcast.6) | data formatting | bytes 262144

commit v4 on v3

--- a/solution.py
+++ b/solution.py
@@ -19,6 +19,8 @@
 OWN = 2 * SLOT
 FORWARD = (5, 9, 14)
 VMEM_ALL = 67_000_000
+SWAP_VMEM = 55_000_000
+FINISH_VMEM = 32_000_000
 CAP = 192
 F32 = jnp.float32
 BF16 = jnp.bfloat16
@@ -473,74 +475,77 @@
     )(x_loc, dy_loc, idx_t, w_router_t, w_gate, w_up, w_down)
 
 
-def tail_kernel(s_hbm, q_hbm, gate_hbm, x_hbm, wr_ref, gx_ref, gr_ref,
-                s_own, s_got, q_all, gate_s, x_all, send, recv, local):
-    core = lax.axis_index("ep")
-
+def swap_kernel(q_ref, s_hbm, q_all, s_got, send, recv, local):
     def copy(ref, into, sem, step):
         return pltpu.make_async_remote_copy(
             src_ref=ref, dst_ref=into, send_sem=send.at[sem], recv_sem=recv.at[sem],
             device_id=peer(step), device_id_type=MESH)
 
-    loads = [pltpu.make_async_copy(ref, into, local.at[n]) for n, (ref, into) in enumerate(
-        ((q_hbm, q_all.at[0]), (gate_hbm, gate_s), (s_hbm.at[0], s_own), (x_hbm, x_all)))]
-    for c in loads[:2]:
-        c.start()
     greet_all()
-    loads[0].wait()
-    copies = [copy(q_all.at[0], q_all.at[k], k, k) for k in range(1, SHARDS)]
+    copies = [copy(q_ref, q_all.at[k], k, k) for k in range(1, SHARDS)]
     for k in (6, 7, 2, 3, 4, 5, 1):
         copies[k - 1].start()
     s_copy = copy(s_hbm.at[1], s_got, 0, 1)
     s_copy.start()
-    for c in loads[2:]:
-        c.start()
+    own = pltpu.make_async_copy(q_ref, q_all.at[0], local)
+    own.start()
+    own.wait()
+    for c in (*copies, s_copy):
+        c.wait_recv()
+    for c in (*copies, s_copy):
+        c.wait_send()
+
+
+def swap(dx_part, q_part):
+    vmem = pl.BlockSpec(memory_space=pltpu.VMEM)
+    hbm = pl.BlockSpec(memory_space=pl.ANY)
+    return pl.pallas_call(
+        swap_kernel,
+        out_shape=(jax.ShapeDtypeStruct((SHARDS, 2, E_LOC, TOK), F32), jax.ShapeDtypeStruct((TOK, D), F32)),
+        in_specs=[vmem, hbm],
+        out_specs=(vmem, hbm),
+        scratch_shapes=[
+            pltpu.SemaphoreType.DMA((SHARDS,)),
+            pltpu.SemaphoreType.DMA((SHARDS,)),
+            pltpu.SemaphoreType.DMA,
+        ],
+        compiler_params=pltpu.CompilerParams(collective_id=1, has_side_effects=True, vmem_limit_bytes=SWAP_VMEM),
+        cost_estimate=pl.CostEstimate(flops=5_000_000_000, bytes_accessed=3_000_000, transcendentals=0),
+        name="swap",
+    )(q_part, dx_part)
+
+
+def finish_kernel(info, s_own, s_got, q_all, gates, x_ref, wr_ref, gx_ref, gr_ref):
     def d_logits(k, n):
         near, far = q_all[k, n], q_all[k + 1, 1 - n]
         low = jnp.concatenate([near, far], axis=0)
         high = jnp.concatenate([far, near], axis=0)
-        q = jnp.where(core == 0, low, high)
-        p = gate_s[k + n]
+        q = jnp.where(info[0] == 0, low, high)
+        p = gates[k + n]
         return (p * (q - jnp.sum(p * q, axis=0, keepdims=True))).astype(BF16)
 
-    loads[1].wait()
-    copies[0].wait_recv()
-    d_log = d_logits(0, 0)
-    du = dot_tn(d_log, wr_ref[...])
-    loads[2].wait()
-    s_copy.wait_recv()
-    gx_ref[...] = (s_own[...] + s_got[...] + du).astype(BF16)
-    loads[3].wait()
-    for k in range(2, SHARDS):
-        copies[k - 1].wait_recv()
-    every = jnp.concatenate([d_log] + [d_logits(k - k % 2, k % 2) for k in range(1, SHARDS)], axis=1)
-    gr_ref[...] = dot_nn(every, x_all[...])
-    s_copy.wait_send()
-    for c in copies:
-        c.wait_send()
-
-
-def tail(dx_part, q_part, gates, x_all, w_router_t):
-    vmem = pl.BlockSpec(memory_space=pltpu.VMEM)
-    hbm = pl.BlockSpec(memory_space=pl.ANY)
+    every = [d_logits(k - k % 2, k % 2) for k in range(SHARDS)]
+    gx_ref[...] = (s_own[0] + s_got[...] + dot_tn(every[0], wr_ref[...])).astype(BF16)
+    gr_ref[...] = dot_nn(jnp.concatenate(every, axis=1), x_ref[...])
+
+
+def finish(info, dx_part, s_got, q_all, gates, x_all, w_router_t):
+    def whole(*shape):
+        return pl.BlockSpec(shape, lambda i, info: (0,) * len(shape))
     return pl.pallas_call(
-        tail_kernel,
+        finish_kernel,
         out_shape=(jax.ShapeDtypeStruct((TOK, D), BF16), jax.ShapeDtypeStruct((EXPERTS, D), F32)),
-        in_specs=[hbm] * 4 + [vmem],
-        out_specs=(vmem, vmem),
-        scratch_shapes=[
-            pltpu.VMEM((TOK, D), F32),
-            pltpu.VMEM((TOK, D), F32),
-            pltpu.VMEM((SHARDS, 2, E_LOC, TOK), F32),
-            pltpu.VMEM((SHARDS, EXPERTS, TOK), F32),
-            pltpu.VMEM((SHARDS * TOK, D), BF16),
-            pltpu.SemaphoreType.DMA((SHARDS,)),
-            pltpu.SemaphoreType.DMA((SHARDS,)),
-            pltpu.SemaphoreType.DMA((4,)),
-        ],
-        compiler_params=pltpu.CompilerParams(collective_id=1, has_side_effects=True, vmem_limit_bytes=62_000_000),
-        name="tail",
-    )(dx_part, q_part, gates, x_all.reshape(SHARDS * TOK, D), w_router_t)
+        grid_spec=pltpu.PrefetchScalarGridSpec(
+            num_scalar_prefetch=1,
+            grid=(1,),
+            in_specs=[whole(1, TOK, D), whole(TOK, D), whole(SHARDS, 2, E_LOC, TOK), whole(SHARDS, EXPERTS, TOK),
+                      whole(SHARDS * TOK, D), whole(EXPERTS, D)],
+            out_specs=(whole(TOK, D), whole(EXPERTS, D)),
+        ),
+        compiler_params=pltpu.CompilerParams(vmem_limit_bytes=FINISH_VMEM),
+        cost_estimate=pl.CostEstimate(flops=1_000_000_000, bytes_accessed=7_000_000, transcendentals=0),
+        name="finish",
+    )(info, dx_part, s_got, q_all, gates, x_all.reshape(SHARDS * TOK, D), w_router_t)
 
 
 def solution(mesh):
@@ -554,7 +559,8 @@
             x_loc, dy_loc, route_idx.T, w_router_t, w_gate, w_up, w_down)
         g1, g3, g2, dx_part, q_part, gates = expert_pass(
             info, x_all, g_all, idx_all, w_router_t, dx_own, q_own, own, w_gate, w_up, w_down)
-        grad_x, grad_router_t = tail(dx_part, q_part, gates, x_all, w_router_t)
+        q_all, s_got = swap(dx_part, q_part)
+        grad_x, grad_router_t = finish(info, dx_part, s_got, q_all, gates, x_all, w_router_t)
         return grad_x, g1, g3, g2, grad_router_t.T
 
     return jax.shard_map(device_step, mesh=mesh, in_specs=(tok_spec, tok_spec, P(), exp_spec, exp_spec, exp_spec, tok_spec), out_specs=(tok_spec, exp_spec, exp_spec, exp_spec, P()), check_vma=False)

time: 148 us -> 145 us (0.980); the launches traced: 148 us -> 143 us
  local copies, waits for them, and re-layouts: 3.44 us -> 0.77 us
  Pallas kernels: 144 us -> 142 us
    pallas_call x1, Pallas kernels: 87.3 us -> 77.3 us  [expert_pass(): pl.pallas_call(main_kernel, out_shape=(jax.ShapeDtypeStruct((E_LOC, D, FF...]
    pallas_call x1 -> x2, Pallas kernels: 9.15 us -> 16.9 us  [the longest x1 15.1 us: swap(): pl.pallas_call(swap_kernel, out_shape=(jax.ShapeDtypeStruct((SHARDS, 2, E...]
    unnamed x2 -> x10, local copies, waits for them, and re-layouts: 3.44 us -> 0.77 us
where the time goes in v4:
time: 145 us; the launch traced here: 143 us
  Pallas kernels  142 us (98%)
    pallas_call x1, Pallas kernels, expert_pass(): pl.pallas_call(main_kernel, out_shape=(jax.ShapeDtypeStruct((E_LOC, D, FF...  77.3 us
    pallas_call x1, Pallas kernels, share_tokens(): pl.pallas_call(share_kernel, out_shape=(jax.ShapeDtypeStruct((SHARDS, TOK...  47.7 us
    pallas_call x1, Pallas kernels, swap(): pl.pallas_call(swap_kernel, out_shape=(jax.ShapeDtypeStruct((SHARDS, 2, E...  15.1 us

profile of v4, /device:TPU:0, one launch (start us, length us, event | category | flops | bytes accessed | tf_op | source)
XLA Modules:
  0.0 143.5 jit_solution(13207232293159580421)
XLA Ops:
  0.6 47.7 %share.1 = (bf16[8,256,1024]{2,1,0:T(8,128)(2,1)}, bf16[8,256,1024]{2,1,0:T(8,128)(2,1)}, s32[8,8,256]{2,1,0:T(8,128)}, f32[2,256,1024]{2,1,0:T(8,128)}, f32[2,1...) custom-call(bf16[256,1024]{1,0:T(8,128)(2,1)} %x_hbm.1, ...), custom_call_target="tpu_custom_call" | custom-call | flops 20000000000 | bytes 70000000 | tf_op jit(solution)/shard_map/share/pallas_call | solution.py:434
  48.4 77.3 %experts.1 = (f32[16,1024,512]{2,1,0:T(8,128)}, f32[16,1024,512]{2,1,0:T(8,128)}, f32[16,512,1024]{2,1,0:T(8,128)}, f32[2,256,1024]{2,1,0:T(8,128)}, f32[2,16,256]{2,1,0:T(8,128)}, /*index=5*/f32[8,32,256]{2,1,0:T(8,128)}) custom-call(s32[1]{0:T(128)} %bitcast.info, bf16[8,256,1024]{2,1,0:T(8,128)(2,1)} %get-tuple-element.25.x_hbm, ...), custom_call_target="tpu_custom_call" | custom-call | flops 70000001024 | bytes 180000000 | tf_op jit(solution)/shard_map/experts/pallas_call | solution.py:228
  125.7 0.0 copy-start.4
  125.7 0.7 copy-done.4
  126.5 0.0 copy-start
  126.5 0.0 copy-start.1
  126.5 0.0 copy-start.2
  126.5 0.0 copy-start.3
  126.5 15.1 %swap.1 = (f32[8,2,16,256]{3,2,1,0:T(8,128)S(1)}, f32[256,1024]{1,0:T(8,128)S(1)}) custom-call(f32[2,16,256]{2,1,0:T(8,128)S(1)} %copy-done.4, f32[2,256,1024]{2,1,0:T(8,128)} %get-tuple-element.35.s_hbm.s_own), custom_call_target="tpu_custom_call" | custom-call | flops 5000000000 | bytes 3000000 | tf_op jit(solution)/shard_map/swap/pallas_call | solution.py:502
  141.6 0.0 copy-done
  141.6 0.0 copy-done.1
  141.7 0.0 copy-done.2
  141.7 0.0 copy-done.3
  141.7 1.8 %finish.1 = (bf16[256,1024]{1,0:T(8,128)(2,1)}, f32[32,1024]{1,0:T(8,128)}) custom-call(s32[1]{0:T(128)} %bitcast.info, f32[2,256,1024]{2,1,0:T(8,128)S(1)} %copy-done.1, f32[256,1024]{1,0:T(8,128)S(1)} %get-tuple-element.37.s_got, f32[8,2,16,256]{3,2,1,0:T(8,128)S(1)} %get-tuple-element.38.q_all, f32[8,32,256]{2,1,0:T(8,128)S(1)} %copy-done.2, ...), custom_call_target="tpu_custom_call" | custom-call | flops 1000000000 | bytes 7000000 | tf_op jit(solution)/shard_map/finish/pallas_call | solution.py:535
Async XLA Ops:
  125.7 0.8 copy-start.4
  126.5 15.2 %copy-start = (bf16[8,256,1024]{2,1,0:T(8,128)(2,1)S(1)}, bf16[8,256,1024]{2,1,0:T(8,128)(2,1)}, u32[]{:S(2)}) copy-start(bf16[8,256,1024]{2,1,0:T(8,128)(2,1)} %get-tuple-element.25.x_hbm) | copy-start | bytes 12582916
  126.5 15.2 %copy-start.1 = (f32[2,256,1024]{2,1,0:T(8,128)S(1)}, f32[2,256,1024]{2,1,0:T(8,128)}, u32[]{:S(2)}) copy-start(f32[2,256,1024]{2,1,0:T(8,128)} %get-tuple-element.35.s_hbm.s_own) | copy-start | bytes 6291460
  126.5 15.2 %copy-start.2 = (f32[8,32,256]{2,1,0:T(8,128)S(1)}, f32[8,32,256]{2,1,0:T(8,128)}, u32[]{:S(2)}) copy-start(f32[8,32,256]{2,1,0:T(8,128)} %get-tuple-element.39.gates) | copy-start | bytes 786436
  126.5 15.2 %copy-start.3 = (bf16[1024,32]{0,1:T(8,128)(2,1)S(1)}, bf16[1024,32]{0,1:T(8,128)(2,1)}, u32[]{:S(2)}) copy-start(bf16[1024,32]{0,1:T(8,128)(2,1)} %param.9) | copy-start | bytes 196612
